TPU v7x, 32 devices: a whole 2x2x4 slice. The times are simulated.
32 devices in a mesh: dp: 8 (over z, x), mp: 4 (over y, core).
Axes of the slice: x: 2, y: 2, z: 4, core: 2. Of those that a mesh axis runs over, the one named last changes fastest.
Arguments:
- hidden: bfloat16 [16, 4608], P('dp'), may hold values from -6 to 6
- in_gain: float32 [1, 4608], replicated, may hold values from 0.5 to 1.5
- post_gain: float32 [1, 4608], replicated, may hold values from 0.5 to 1.5
- query_weight: bfloat16 [1, 4608, 2048], P(None, 'dp', 'mp'), may hold values from -0.09375 to 0.09375
- key_weight: bfloat16 [1, 4608, 1024], P(None, 'dp', 'mp'), may hold values from -0.09375 to 0.09375
- value_weight: bfloat16 [1, 4608, 1024], P(None, 'dp', 'mp'), may hold values from -0.09375 to 0.09375
- out_weight: bfloat16 [1, 2048, 4608], P(None, 'mp', 'dp'), may hold values from -0.125 to 0.125
- key_cache: bfloat16 [1, 16, 512, 8, 128], P(None, 'dp', 'mp'), may hold values from -6 to 6
- value_cache: bfloat16 [1, 16, 512, 8, 128], P(None, 'dp', 'mp'), may hold values from -6 to 6
- lengths: int32 [16], P('dp'), may hold values from 256 to 512
- windowed: int32 [1, 16], P(None, 'dp'), may hold values from 0 to 1
Outputs:
- hidden_out: bfloat16 [16, 4608], P('dp')
- new_keys: bfloat16 [1, 16, 8, 128], P(None, 'dp')
- new_values: bfloat16 [1, 16, 8, 128], P(None, 'dp')
Inputs may be any that keep to these rules, and one draw needn't show every extreme that they name: `lengths`: every request has between 256 and 512 cached tokens. `windowed`: each flag is 0 or 1, for every layer and request.
All inputs are finite; a program needn't handle non-finite values.
Results may differ from a plain program's by a relative error of at most 0.008.
Values may be sent and summed in bfloat16 or wider, within the bound.
A program may use at most 64 MiB of HBM per device.

v0:
```python
import jax
import jax.numpy as jnp
from jax import lax
from jax.sharding import PartitionSpec as P

HEADS = 16
KV_HEADS = 8
HEAD_DIM = 128
LAYERS = 1


EPSILON = 1e-06
SOFTCAP = 50.0
ROPE_BASE = 10000.0
NEGATIVE = -1e30


def rms_scale(values, gain_row):
    values = values.astype(jnp.float32)
    mean_square = jnp.mean(values * values, axis=-1, keepdims=True)
    return values * lax.rsqrt(mean_square + EPSILON) * gain_row.astype(jnp.float32)


def rotate(values, positions):
    half_dim = values.shape[-1] // 2
    frequency = jnp.power(
        ROPE_BASE, -2.0 * jnp.arange(half_dim, dtype=jnp.float32) / values.shape[-1]
    )
    angles = positions.astype(jnp.float32)[:, None] * frequency[None, :]
    cosine = jnp.cos(angles)[:, None, :]
    sine_table = jnp.sin(angles)[:, None, :]
    front_half = values[..., :half_dim]
    back_half = values[..., half_dim:]
    return jnp.concatenate(
        (
            front_half * cosine - back_half * sine_table,
            back_half * cosine + front_half * sine_table,
        ),
        axis=-1,
    )


def on_device(
    hidden,
    in_gain,
    post_gain,
    query_weight,
    key_weight,
    value_weight,
    out_weight,
    key_cache,
    value_cache,
    lengths,
    windowed,
):
    row_count = hidden.shape[0]
    query_width = query_weight.shape[2]
    key_width = key_weight.shape[2]
    seq_block = key_cache.shape[2]
    head_width = out_weight.shape[1]
    group_size = HEADS // KV_HEADS
    window_len = seq_block * lax.axis_size("mp") // 2
    keys_out = []
    values_out = []
    for layer_index in range(LAYERS):
        normed = rms_scale(hidden, in_gain[layer_index]).astype(jnp.bfloat16)
        token_slab = lax.all_to_all(normed, "dp", split_axis=1, concat_axis=0, tiled=True)
        joined = jnp.concatenate(
            (query_weight[layer_index], key_weight[layer_index], value_weight[layer_index]), 1
        )

        def local_term():
            part_rows = lax.slice_in_dim(token_slab, 0, row_count * lax.axis_size("dp"), axis=0)
            return jnp.dot(part_rows, joined, preferred_element_type=jnp.float32)

        summed = lax.psum_scatter(local_term(), "dp", scatter_dimension=0, tiled=True)
        query_part = summed[:, :query_width]
        key_part = summed[:, query_width : query_width + key_width]
        value_part = summed[:, query_width + key_width :]
        rounded = (
            query_part.astype(jnp.bfloat16),
            key_part.astype(jnp.bfloat16),
            value_part.astype(jnp.bfloat16),
        )
        query, key_raw, value_new = (
            lax.all_gather(rounded[0], "mp", axis=1, tiled=True),
            lax.all_gather(rounded[1], "mp", axis=1, tiled=True),
            lax.all_gather(rounded[2], "mp", axis=1, tiled=True),
        )
        queries = rotate(query.astype(jnp.float32).reshape(row_count, HEADS, HEAD_DIM), lengths)
        queries = (queries * HEAD_DIM ** (-0.5)).astype(jnp.bfloat16)
        keys_new = rotate(
            key_raw.astype(jnp.float32).reshape(row_count, KV_HEADS, HEAD_DIM), lengths
        ).astype(jnp.bfloat16)
        value_new = value_new.reshape(row_count, KV_HEADS, HEAD_DIM)
        grouped = queries.reshape(row_count, KV_HEADS, group_size, HEAD_DIM)
        scores = jnp.einsum(
            "rkgd,rskd->rkgs", grouped, key_cache[layer_index], preferred_element_type=jnp.float32
        )
        scores = SOFTCAP * jnp.tanh(scores / SOFTCAP)
        positions = lax.axis_index("mp") * seq_block + jnp.arange(seq_block, dtype=jnp.int32)
        window_flag = windowed[layer_index][:, None]
        usable = (positions[None, :] < lengths[:, None]) & (
            (window_flag == 0) | (positions[None, :] > lengths[:, None] - window_len)
        )
        usable = usable[:, None, None, :]
        masked = jnp.where(usable, scores, NEGATIVE)
        peaks = jnp.max(masked, axis=-1)
        exp_scores = jnp.where(usable, jnp.exp(masked - peaks[..., None]), 0.0)
        sums_exp = jnp.sum(exp_scores, axis=-1)
        accumulated = jnp.einsum(
            "rkgs,rskd->rkgd",
            exp_scores,
            value_cache[layer_index].astype(jnp.float32),
            preferred_element_type=jnp.float32,
        )
        global_peak = lax.pmax(peaks, "mp")
        rescale = jnp.exp(peaks - global_peak)
        sums_exp, accumulated = lax.psum(
            (sums_exp * rescale, accumulated * rescale[..., None]), "mp"
        )
        peaks = global_peak
        self_score = jnp.einsum(
            "rkgd,rkd->rkg", grouped, keys_new, preferred_element_type=jnp.float32
        )
        self_score = SOFTCAP * jnp.tanh(self_score / SOFTCAP)
        peak_all = jnp.maximum(peaks, self_score)
        old_scale = jnp.exp(peaks - peak_all)
        self_weight = jnp.exp(self_score - peak_all)
        denominator = sums_exp * old_scale + self_weight
        mixed = (
            accumulated * old_scale[..., None]
            + self_weight[..., None] * value_new.astype(jnp.float32)[:, :, None, :]
        )
        attended = (
            (mixed / denominator[..., None])
            .reshape(row_count, HEADS * HEAD_DIM)
            .astype(jnp.bfloat16)
        )
        attended_local = lax.dynamic_slice_in_dim(
            attended, lax.axis_index("mp") * head_width, head_width, 1
        )
        all_rows = lax.all_gather(attended_local, "dp", axis=0, tiled=True)
        partial_cols = jnp.dot(
            all_rows, out_weight[layer_index], preferred_element_type=jnp.float32
        )
        partial_cols = lax.psum(partial_cols, "mp")
        projected = lax.all_to_all(partial_cols, "dp", split_axis=0, concat_axis=1, tiled=True)
        hidden = (hidden.astype(jnp.float32) + rms_scale(projected, post_gain[layer_index])).astype(
            jnp.bfloat16
        )
        keys_out.append(keys_new)
        values_out.append(value_new)
    return (hidden, jnp.stack(keys_out), jnp.stack(values_out))


def solution(mesh):
    return jax.shard_map(
        on_device,
        mesh=mesh,
        in_specs=(
            P("dp", None),
            P(),
            P(),
            P(None, "dp", "mp"),
            P(None, "dp", "mp"),
            P(None, "dp", "mp"),
            P(None, "mp", "dp"),
            P(None, "dp", "mp", None, None),
            P(None, "dp", "mp", None, None),
            P("dp"),
            P(None, "dp"),
        ),
        out_specs=(P("dp", None), P(None, "dp", None, None), P(None, "dp", None, None)),
        check_vma=False,
    )
```

profile of v0, /device:TPU:0, one launch (start us, length us, event | category | flops | bytes accessed | tf_op | source)
XLA Modules:
  0.0 144.0 jit_solution(18006181525195604881)
XLA Ops:
  0.6 0.9 fusion.13
  1.6 0.8 reduce.1
  2.4 0.8 fusion.15
  3.3 0.6 copy.21
  3.9 7.3 %all-to-all-start = ((bf16[2,8,576]{2,0,1:T(2,128)(2,1)}), bf16[2,8,576]{2,0,1:T(2,128)(2,1)S(1)}, u32[]{:S(2)}, u32[]{:S(2)}) async-start(bf16[2,8,576]{2,0,1:T(2,128)(2,1)} %copy.21), calls=%async_computation | async-start | bytes 40960 | tf_op jit(solution)/shard_map/all_to_all | solution.py:67
  11.2 0.7 compare_bitcast_fusion
  11.9 0.7 broadcast_add_fusion
  12.7 0.7 or_and_fusion
  13.5 0.8 reduce.2
  14.3 1.2 dynamic-slice
  16.1 1.7 %all-to-all-done = bf16[2,8,576]{2,0,1:T(2,128)(2,1)S(1)} async-done(((bf16[2,8,576]{2,0,1:T(2,128)(2,1)}), bf16[2,8,576]{2,0,1:T(2,128)(2,1)S(1)}, u32[]{:S(2)}, u32[]{:S(2)}) %all-to-all-start) | async-done | bytes 18464 | tf_op jit(solution)/shard_map/all_to_all | solution.py:67
  17.9 1.6 %fusion = f32[16,1024]{1,0:T(8,128)S(1)} fusion(bf16[16,576]{1,0:T(8,128)(2,1)S(1)} %all_to_all.31, bf16[576,256]{1,0:T(8,128)(2,1)} %bitcast.62, bf16[576,256]{1,0:T(8,128)(2,1)} %bitcast.63, bf16[576,512]{1,0:T(8,128)(2,1)} %bitcast.59), kind=kOutput, calls=%fused_computation | convolution fusion | flops 22413312 | bytes 1263616 | tf_op jit(solution)/shard_map/dot_general | solution.py:74
  19.4 36.5 %all-reduce = bf16[16,1024]{1,0:T(8,128)(2,1)S(1)} all-reduce(f32[16,1024]{1,0:T(8,128)S(1)} %fusion), channel_id=2, replica_groups=mesh['dp'=8,'mp'=4] {'dp'}, use_global_device_ids=true, to_apply=%region_1.0.clone | all-reduce | flops 16384 | bytes 98304
  56.0 5.1 %all_gather.14 = bf16[2,1024]{1,0:T(2,128)(2,1)S(1)} all-gather(bf16[2,256]{1,0:T(2,128)(2,1)S(1)} %get-tuple-element.14), channel_id=1, replica_groups=mesh['dp'=8,'mp'=4] {'mp'}, dimensions={1}, use_global_device_ids=true | all-gather | bytes 5120 | tf_op jit(solution)/shard_map/all_gather | solution.py:88
  61.6 5.1 %all_gather.13 = bf16[2,1024]{1,0:T(2,128)(2,1)S(1)} all-gather(bf16[2,256]{1,0:T(2,128)(2,1)S(1)} %get-tuple-element.15), channel_id=1, replica_groups=mesh['dp'=8,'mp'=4] {'mp'}, dimensions={1}, use_global_device_ids=true | all-gather | bytes 5120 | tf_op jit(solution)/shard_map/all_gather | solution.py:87
  66.7 5.2 %all_gather.12 = bf16[2,2048]{1,0:T(2,128)(2,1)S(1)} all-gather(bf16[2,512]{1,0:T(2,128)(2,1)S(1)} %slice.31), channel_id=1, replica_groups=mesh['dp'=8,'mp'=4] {'mp'}, dimensions={1}, use_global_device_ids=true | all-gather | bytes 10240 | tf_op jit(solution)/shard_map/all_gather | solution.py:86
  72.8 7.2 %pmax.7 = f32[2,8,2]{2,1,0:T(8,128)S(1)} all-reduce(f32[2,8,2]{2,1,0:T(8,128)S(1)} %get-tuple-element.20), channel_id=1, replica_groups=mesh['dp'=8,'mp'=4] {'mp'}, use_global_device_ids=true, to_apply=%region_3.4 | all-reduce | flops 32 | bytes 256 | tf_op jit(solution)/shard_map/pmax | solution.py:117
  80.5 10.3 %all-reduce.1 = (f32[2,8,2,128]{3,2,1,0:T(2,128)S(1)}, f32[2,8,2]{2,1,0:T(8,128)S(1)}) all-reduce(f32[2,8,2,128]{3,2,1,0:T(2,128)S(1)} %convolution_multiply_fusion, f32[2,8,2]{2,1,0:T(8,128)S(1)} %get-tuple-element.8), channel_id=1, replica_groups=mesh['dp'=8,'mp'=4] {'mp'}, use_global_device_ids=true, to_apply=%region_4.5 | all-reduce | flops 4128 | bytes 33024 | tf_op jit(solution)/shard_map/psum | solution.py:119
  91.1 30.4 %all-gather = bf16[8,2,512]{2,1,0:T(2,128)(2,1)S(1)} all-gather(bf16[1,2,512]{2,1,0:T(2,128)(2,1)S(1)} %dynamic-slice_bitcast_fusion), channel_id=1, replica_groups=mesh['dp'=8,'mp'=4] {'dp'}, dimensions={0}, use_global_device_ids=true | all-gather | bytes 18432 | tf_op jit(solution)/shard_map/all_gather | solution.py:143
  121.9 11.2 %psum.23 = f32[8,2,576]{2,1,0:T(2,128)} all-reduce(f32[8,2,576]{2,1,0:T(2,128)S(1)} %all_to_all.32), channel_id=1, replica_groups=mesh['dp'=8,'mp'=4] {'mp'}, use_global_device_ids=true, to_apply=%region_7.8 | all-reduce | flops 9216 | bytes 73728 | tf_op jit(solution)/shard_map/psum | solution.py:147
  133.0 3.3 %all-to-all-start.1 = ((f32[8,2,576]{2,1,0:T(2,128)}), f32[8,2,576]{2,1,0:T(2,128)S(1)}, u32[]{:S(2)}, u32[]{:S(2)}) async-start(f32[8,2,576]{2,1,0:T(2,128)} %psum.23), calls=%async_computation.1 | async-start | bytes 81920 | tf_op jit(solution)/shard_map/all_to_all | solution.py:148
  136.4 0.7 pad_maximum_fusion
  137.0 6.0 %all-to-all-done.1 = f32[8,2,576]{2,1,0:T(2,128)S(1)} async-done(((f32[8,2,576]{2,1,0:T(2,128)}), f32[8,2,576]{2,1,0:T(2,128)S(1)}, u32[]{:S(2)}, u32[]{:S(2)}) %all-to-all-start.1) | async-done | bytes 36896 | tf_op jit(solution)/shard_map/all_to_all | solution.py:148
  143.3 0.7 fusion.16
  (44 shorter events, 3.0 us)
Async XLA Ops:
  0.6 120.9 %copy-start = (bf16[1,512,576]{1,2,0:T(8,128)(2,1)S(1)}, bf16[1,512,576]{1,2,0:T(8,128)(2,1)}, u32[]{:S(2)}) copy-start(bf16[1,512,576]{1,2,0:T(8,128)(2,1)} %param.17) | copy-start | bytes 1769476
  3.9 13.9 %all-to-all-start = ((bf16[2,8,576]{2,0,1:T(2,128)(2,1)}), bf16[2,8,576]{2,0,1:T(2,128)(2,1)S(1)}, u32[]{:S(2)}, u32[]{:S(2)}) async-start(bf16[2,8,576]{2,0,1:T(2,128)(2,1)} %copy.21), calls=%async_computation | async-start | bytes 40960 | tf_op jit(solution)/shard_map/all_to_all | solution.py:67
  17.8 54.5 %copy-start.2 = (bf16[1,2,128,8,128]{4,3,2,1,0:T(8,128)(2,1)S(1)}, bf16[1,2,128,8,128]{4,3,2,1,0:T(8,128)(2,1)}, u32[]{:S(2)}) copy-start(bf16[1,2,128,8,128]{4,3,2,1,0:T(8,128)(2,1)} %param.18) | copy-start | bytes 1572868
  19.4 60.8 %copy-start.3 = (bf16[1,2,128,8,128]{4,3,2,1,0:T(8,128)(2,1)S(1)}, bf16[1,2,128,8,128]{4,3,2,1,0:T(8,128)(2,1)}, u32[]{:S(2)}) copy-start(bf16[1,2,128,8,128]{4,3,2,1,0:T(8,128)(2,1)} %param.19) | copy-start | bytes 1572868
  91.0 52.3 %copy-start.1 = (bf16[2,4608]{1,0:T(2,128)(2,1)S(1)}, bf16[2,4608]{1,0:T(2,128)(2,1)}, u32[]{:S(2)}) copy-start(bf16[2,4608]{1,0:T(2,128)(2,1)} %param.11) | copy-start | bytes 55300
  133.0 10.0 %all-to-all-start.1 = ((f32[8,2,576]{2,1,0:T(2,128)}), f32[8,2,576]{2,1,0:T(2,128)S(1)}, u32[]{:S(2)}, u32[]{:S(2)}) async-start(f32[8,2,576]{2,1,0:T(2,128)} %psum.23), calls=%async_computation.1 | async-start | bytes 81920 | tf_op jit(solution)/shard_map/all_to_all | solution.py:148
where the time goes:
time: 145 us; the launch traced here: 144 us
  blocking collectives  111 us (77%)
  starting transfers between devices  10.7 us (7%)
  other arithmetic  7.74 us (5%)
  waiting for transfers between devices  7.67 us (5%)
  local copies, waits for them, and re-layouts  2.81 us (2%)
  matrix products  2.7 us (2%)
  between operations  1.49 us (1%)
    unnamed x1, blocking collectives  36.5 us
    all_gather x1, blocking collectives, on_device(): all_rows = lax.all_gather(attended_local, 'dp', axis=0, tiled=True)  30.4 us
    psum x1, blocking collectives, on_device(): partial_cols = lax.psum(partial_cols, 'mp')  11.2 us
    psum x1, blocking collectives, on_device(): lax.psum((sums_exp * rescale, accumulated * rescale[..., None]), 'mp')  10.3 us
    all_to_all x1, starting transfers between devices, on_device(): lax.all_to_all(normed, 'dp', split_axis=1, concat_axis=0, tiled=True)  7.31 us
    pmax x1, blocking collectives, on_device(): global_peak = lax.pmax(peaks, 'mp')  7.24 us
    all_to_all x1, waiting for transfers between devices, on_device(): lax.all_to_all(partial_cols, 'dp', split_axis=0, concat_axis=1, tiled=True)  6.01 us
    all_gather x1, blocking collectives, on_device(): lax.all_gather(rounded[0], 'mp', axis=1, tiled=True)  5.15 us
  transfers between devices with their start and end apart: 2, of which 2 were waited for; matrix products, arithmetic and copies ran while one was open for 3% of the time, Pallas kernels for 0%

commit v1 on v0

--- a/solution.py
+++ b/solution.py
@@ -1,6 +1,11 @@
+import functools
+import math
+
 import jax
 import jax.numpy as jnp
 from jax import lax
+from jax.experimental import pallas as pl
+from jax.experimental.pallas import tpu as pltpu
 from jax.sharding import PartitionSpec as P
 
 HEADS = 16
@@ -154,9 +159,390 @@
     return (hidden, jnp.stack(keys_out), jnp.stack(values_out))
 
 
+MESH_ID = pl.DeviceIdType.MESH
+BLOCK_ROWS = 8
+
+
+def fits(mesh):
+    parts = mesh.shape["mp"]
+    query_heads = HEADS // parts
+    key_heads = KV_HEADS // parts
+    return (
+        HEADS % parts == 0
+        and KV_HEADS % parts == 0
+        and query_heads == 2 * key_heads
+        and query_heads + 2 * key_heads == BLOCK_ROWS
+    )
+
+
+def one_hot(rows, columns, match):
+    row = lax.broadcasted_iota(jnp.int32, (rows, columns), 0)
+    column = lax.broadcasted_iota(jnp.int32, (rows, columns), 1)
+    return jnp.where(match(row, column), 1.0, 0.0).astype(jnp.bfloat16)
+
+
+def pick(selector, values):
+    return jnp.dot(selector, values, preferred_element_type=jnp.float32)
+
+
+def fused_kernel(
+    dp,
+    mp,
+    lengths_ref,
+    windowed_ref,
+    hidden_ref,
+    in_gain_ref,
+    post_gain_ref,
+    query_hbm,
+    key_hbm,
+    value_hbm,
+    out_hbm,
+    key_cache_hbm,
+    value_cache_hbm,
+    hidden_out_ref,
+    new_keys_ref,
+    new_values_ref,
+    query_w,
+    key_w,
+    value_w,
+    out_w,
+    keys,
+    values,
+    norm_send,
+    norm_recv,
+    proj_send,
+    proj_recv,
+    mix_send,
+    mix_recv,
+    cols_send,
+    cols_recv,
+    load_sem,
+    send_sem,
+    recv_sem,
+):
+    my_dp = lax.axis_index("dp")
+    my_mp = lax.axis_index("mp")
+    devices = dp * mp
+    me = my_dp * mp + my_mp
+    rows = hidden_ref.shape[0]
+    total_rows = rows * dp
+    slab = norm_send.shape[2]
+    query_width = query_w.shape[1]
+    key_width = key_w.shape[1]
+    query_heads = query_width // HEAD_DIM
+    key_heads = key_width // HEAD_DIM
+    seq_block = key_cache_hbm.shape[2]
+    cache_rows = seq_block * KV_HEADS
+    window_len = seq_block * mp // 2
+
+    loads = [
+        pltpu.make_async_copy(src, dst, load_sem.at[i])
+        for i, (src, dst) in enumerate(
+            (
+                (query_hbm.at[0], query_w),
+                (key_hbm.at[0], key_w),
+                (value_hbm.at[0], value_w),
+                (key_cache_hbm.at[0], keys),
+                (value_cache_hbm.at[0], values),
+                (out_hbm.at[0], out_w),
+            )
+        )
+    ]
+    barrier = pltpu.get_barrier_semaphore()
+    for step in range(1, devices):
+        there = lax.rem(me + step, devices)
+        pl.semaphore_signal(
+            barrier,
+            inc=1,
+            device_id={"dp": there // mp, "mp": lax.rem(there, mp)},
+            device_id_type=MESH_ID,
+        )
+    for load in loads:
+        load.start()
+
+    hidden = hidden_ref[...].astype(jnp.float32)
+    mean_square = jnp.mean(hidden * hidden, axis=-1, keepdims=True)
+    normed = hidden * lax.rsqrt(mean_square + EPSILON) * in_gain_ref[...]
+    for part in range(dp):
+        norm_send[part] = normed[:, part * slab : (part + 1) * slab].astype(jnp.bfloat16)
+    norm_recv[my_dp] = norm_send[my_dp]
+
+    pl.semaphore_wait(barrier, devices - 1)
+    for step in range(1, dp):
+        there = lax.rem(my_dp + step, dp)
+        pltpu.make_async_remote_copy(
+            src_ref=norm_send.at[there],
+            dst_ref=norm_recv.at[my_dp],
+            send_sem=send_sem.at[0],
+            recv_sem=recv_sem.at[0],
+            device_id={"dp": there, "mp": my_mp},
+            device_id_type=MESH_ID,
+        ).start()
+
+    def finish(buffer, count, sem):
+        block = buffer.at[pl.ds(0, count)]
+        pltpu.make_async_copy(block, block, sem).wait()
+
+    def scatter(send, recv, stage, slot_of):
+        for step in range(1, devices):
+            there = lax.rem(me + step, devices)
+            there_dp = there // mp
+            there_mp = lax.rem(there, mp)
+            pltpu.make_async_remote_copy(
+                src_ref=send.at[slot_of(there_dp, there_mp)],
+                dst_ref=recv.at[me],
+                send_sem=send_sem.at[stage],
+                recv_sem=recv_sem.at[stage],
+                device_id={"dp": there_dp, "mp": there_mp},
+                device_id_type=MESH_ID,
+            ).start()
+        recv[me] = send[slot_of(my_dp, my_mp)]
+
+    lane = lax.broadcasted_iota(jnp.int32, (BLOCK_ROWS, HEAD_DIM), 1)
+    half = HEAD_DIM // 2
+    pair = jnp.where(lane < half, lane, lane - half).astype(jnp.float32)
+    frequency = jnp.exp(pair * (-2.0 / HEAD_DIM * math.log(ROPE_BASE)))
+    cosines = []
+    sines = []
+    for r in range(rows):
+        angle = lengths_ref[r].astype(jnp.float32) * frequency
+        cosines.append(jnp.cos(angle))
+        sine = jnp.sin(angle)
+        sines.append(jnp.where(lane < half, -sine, sine))
+
+    for load in loads[:3]:
+        load.wait()
+    finish(norm_recv, dp - 1, recv_sem.at[0])
+    tokens = jnp.concatenate(
+        [norm_recv[part].astype(jnp.float32) for part in range(dp)], axis=0
+    ).astype(jnp.bfloat16)
+    parts = [
+        jnp.dot(tokens, weight[...], preferred_element_type=jnp.float32)
+        for weight in (query_w, key_w, value_w)
+    ]
+    pieces = []
+    for part in parts:
+        for at in range(0, part.shape[1], HEAD_DIM):
+            pieces.append(part[:, at : at + HEAD_DIM])
+    stacked = jnp.concatenate(pieces, axis=0).astype(jnp.bfloat16)
+    spread = one_hot(
+        total_rows * BLOCK_ROWS,
+        total_rows * BLOCK_ROWS,
+        lambda row, column: column
+        == (row % BLOCK_ROWS) * total_rows + row // BLOCK_ROWS,
+    )
+    proj_send[...] = (
+        pick(spread, stacked).astype(jnp.bfloat16).reshape(dp, rows * BLOCK_ROWS, HEAD_DIM)
+    )
+    scatter(proj_send, proj_recv, 1, lambda there_dp, there_mp: there_dp)
+
+    for load in loads[3:5]:
+        load.wait()
+    group_rows = mp * BLOCK_ROWS
+    row = lax.broadcasted_iota(jnp.int32, (group_rows, cache_rows), 0)
+    column = lax.broadcasted_iota(jnp.int32, (group_rows, cache_rows), 1)
+    in_block = row % BLOCK_ROWS
+    head_match = (in_block < query_heads) & (
+        column % KV_HEADS == (row // BLOCK_ROWS) * key_heads + in_block // 2
+    )
+    position = my_mp * seq_block + column // KV_HEADS
+    allowed = []
+    for r in range(rows):
+        length = lengths_ref[r]
+        floor = jnp.where(windowed_ref[0, r] == 0, -1, length - window_len)
+        allowed.append(head_match & (position < length) & (position > floor))
+    self_row = lax.broadcasted_iota(jnp.int32, (group_rows, group_rows), 0)
+    self_column = lax.broadcasted_iota(jnp.int32, (group_rows, group_rows), 1)
+    self_slot = self_row % BLOCK_ROWS
+    own_base = (self_row // BLOCK_ROWS) * BLOCK_ROWS + query_heads + self_slot // 2
+    is_query = self_slot < query_heads
+    self_key = is_query & (self_column == own_base)
+    self_value = jnp.where(is_query & (self_column == own_base + key_heads), 1.0, 0.0).astype(
+        jnp.bfloat16
+    )
+    acc_row = lax.broadcasted_iota(jnp.int32, (group_rows, HEAD_DIM), 0) % BLOCK_ROWS
+    self_share = jnp.where(my_mp == 0, 1.0, 0.0)
+
+    finish(proj_recv, devices - 1, recv_sem.at[1])
+    blocks = rows * BLOCK_ROWS
+    summed = jnp.sum(
+        proj_recv[...].astype(jnp.float32).reshape(dp, mp, blocks, HEAD_DIM), axis=0
+    )
+    rotated_rows = []
+    raw_rows = []
+    for r in range(rows):
+        raw = summed[:, r * BLOCK_ROWS : (r + 1) * BLOCK_ROWS, :].reshape(group_rows, HEAD_DIM)
+        raw = raw.astype(jnp.bfloat16)
+        wide = raw.astype(jnp.float32)
+        cosine = jnp.concatenate([cosines[r]] * mp, axis=0)
+        sine = jnp.concatenate([sines[r]] * mp, axis=0)
+        turned = wide * cosine + pltpu.roll(wide, half, 1) * sine
+        queries = (turned * HEAD_DIM ** (-0.5)).astype(jnp.bfloat16)
+        turned = turned.astype(jnp.bfloat16)
+        rotated_rows.append(turned)
+        raw_rows.append(raw)
+        flat_keys = keys[r].reshape(cache_rows, HEAD_DIM)
+        flat_values = values[r].reshape(cache_rows, HEAD_DIM)
+        over_last = (((1,), (1,)), ((), ()))
+        scores = lax.dot_general(
+            queries, flat_keys, over_last, preferred_element_type=jnp.float32
+        )
+        scores = SOFTCAP * jnp.tanh(scores / SOFTCAP)
+        exp_scores = jnp.where(allowed[r], jnp.exp(scores), 0.0)
+        sums_exp = jnp.sum(exp_scores, axis=-1, keepdims=True)
+        accumulated = jnp.dot(
+            exp_scores.astype(jnp.bfloat16), flat_values, preferred_element_type=jnp.float32
+        )
+        own = lax.dot_general(queries, turned, over_last, preferred_element_type=jnp.float32)
+        own = jnp.sum(jnp.where(self_key, own, 0.0), axis=-1, keepdims=True)
+        own = jnp.exp(SOFTCAP * jnp.tanh(own / SOFTCAP)) * self_share
+        accumulated = accumulated + own * pick(self_value, raw)
+        sums_exp = jnp.broadcast_to(sums_exp + own, (group_rows, HEAD_DIM))
+        message = jnp.where(
+            acc_row < query_heads, accumulated, pltpu.roll(sums_exp, query_heads, 0)
+        )
+        mix_send[:, r * BLOCK_ROWS : (r + 1) * BLOCK_ROWS, :] = message.reshape(
+            mp, BLOCK_ROWS, HEAD_DIM
+        ).astype(mix_send.dtype)
+    scatter(mix_send, mix_recv, 2, lambda there_dp, there_mp: there_mp)
+
+    turned_all = jnp.concatenate(rotated_rows, axis=0)
+    raw_all = jnp.concatenate(raw_rows, axis=0)
+
+    def owner(row, first):
+        head = row % KV_HEADS
+        return (
+            (row // KV_HEADS) * group_rows
+            + (head // key_heads) * BLOCK_ROWS
+            + first
+            + head % key_heads
+        )
+
+    key_rows = one_hot(
+        rows * KV_HEADS, rows * group_rows, lambda row, column: column == owner(row, query_heads)
+    )
+    value_rows = one_hot(
+        rows * KV_HEADS,
+        rows * group_rows,
+        lambda row, column: column == owner(row, query_heads + key_heads),
+    )
+    new_keys_ref[...] = (
+        pick(key_rows, turned_all).astype(jnp.bfloat16).reshape(new_keys_ref.shape)
+    )
+    new_values_ref[...] = (
+        pick(value_rows, raw_all).astype(jnp.bfloat16).reshape(new_values_ref.shape)
+    )
+    gather = one_hot(
+        query_heads * total_rows,
+        total_rows * BLOCK_ROWS,
+        lambda row, column: column
+        == (row % total_rows) * BLOCK_ROWS + row // total_rows,
+    )
+
+    loads[5].wait()
+    finish(mix_recv, devices - 1, recv_sem.at[2])
+    mixed = jnp.sum(
+        mix_recv[...].astype(jnp.float32).reshape(dp, mp, blocks, HEAD_DIM), axis=1
+    ).reshape(dp * blocks, HEAD_DIM)
+    all_row = lax.broadcasted_iota(jnp.int32, mixed.shape, 0) % BLOCK_ROWS
+    weights = pltpu.roll(mixed, mixed.shape[0] - query_heads, 0)
+    attended = jnp.where(all_row < query_heads, mixed / weights, 0.0).astype(jnp.bfloat16)
+    heads = pick(gather, attended).astype(jnp.bfloat16)
+    heads = jnp.concatenate(
+        [heads[b * total_rows : (b + 1) * total_rows] for b in range(query_heads)], axis=1
+    )
+    partial_cols = jnp.dot(heads, out_w[...], preferred_element_type=jnp.float32)
+    for part in range(dp):
+        cols_send[part] = partial_cols[part * rows : (part + 1) * rows].astype(cols_send.dtype)
+    scatter(cols_send, cols_recv, 3, lambda there_dp, there_mp: there_dp)
+    finish(cols_recv, devices - 1, recv_sem.at[3])
+    pieces = []
+    for part in range(dp):
+        piece = cols_recv[part * mp].astype(jnp.float32)
+        for other in range(1, mp):
+            piece = piece + cols_recv[part * mp + other].astype(jnp.float32)
+        pieces.append(piece)
+    projected = jnp.concatenate(pieces, axis=1)
+    mean_square = jnp.mean(projected * projected, axis=-1, keepdims=True)
+    update = projected * lax.rsqrt(mean_square + EPSILON) * post_gain_ref[...]
+    hidden_out_ref[...] = (hidden_ref[...].astype(jnp.float32) + update).astype(jnp.bfloat16)
+
+    finish(norm_recv, dp - 1, send_sem.at[0])
+    finish(proj_recv, devices - 1, send_sem.at[1])
+    finish(mix_recv, devices - 1, send_sem.at[2])
+    finish(cols_recv, devices - 1, send_sem.at[3])
+
+
+def fused_device(
+    hidden,
+    in_gain,
+    post_gain,
+    query_weight,
+    key_weight,
+    value_weight,
+    out_weight,
+    key_cache,
+    value_cache,
+    lengths,
+    windowed,
+):
+    dp = lax.axis_size("dp")
+    mp = lax.axis_size("mp")
+    rows = hidden.shape[0]
+    slab = query_weight.shape[1]
+    out_slab = out_weight.shape[2]
+    blocks = rows * BLOCK_ROWS
+    half_word = jnp.bfloat16
+    smem = pl.BlockSpec(memory_space=pltpu.SMEM)
+    vmem = pl.BlockSpec(memory_space=pltpu.VMEM)
+    far = pl.BlockSpec(memory_space=pl.ANY)
+    return pl.pallas_call(
+        functools.partial(fused_kernel, dp, mp),
+        out_shape=(
+            jax.ShapeDtypeStruct(hidden.shape, half_word),
+            jax.ShapeDtypeStruct((LAYERS, rows, KV_HEADS, HEAD_DIM), half_word),
+            jax.ShapeDtypeStruct((LAYERS, rows, KV_HEADS, HEAD_DIM), half_word),
+        ),
+        in_specs=[smem, smem, vmem, vmem, vmem, far, far, far, far, far, far],
+        out_specs=(vmem, vmem, vmem),
+        scratch_shapes=[
+            pltpu.VMEM(query_weight.shape[1:], half_word),
+            pltpu.VMEM(key_weight.shape[1:], half_word),
+            pltpu.VMEM(value_weight.shape[1:], half_word),
+            pltpu.VMEM(out_weight.shape[1:], half_word),
+            pltpu.VMEM(key_cache.shape[1:], half_word),
+            pltpu.VMEM(value_cache.shape[1:], half_word),
+            pltpu.VMEM((dp, rows, slab), half_word),
+            pltpu.VMEM((dp, rows, slab), half_word),
+            pltpu.VMEM((dp, blocks, HEAD_DIM), half_word),
+            pltpu.VMEM((dp * mp, blocks, HEAD_DIM), half_word),
+            pltpu.VMEM((mp, blocks, HEAD_DIM), half_word),
+            pltpu.VMEM((dp * mp, blocks, HEAD_DIM), half_word),
+            pltpu.VMEM((dp, rows, out_slab), half_word),
+            pltpu.VMEM((dp * mp, rows, out_slab), half_word),
+            pltpu.SemaphoreType.DMA((6,)),
+            pltpu.SemaphoreType.DMA((4,)),
+            pltpu.SemaphoreType.DMA((4,)),
+        ],
+        compiler_params=pltpu.CompilerParams(collective_id=0, has_side_effects=True),
+    )(
+        lengths,
+        windowed,
+        hidden,
+        in_gain,
+        post_gain,
+        query_weight,
+        key_weight,
+        value_weight,
+        out_weight,
+        key_cache,
+        value_cache,
+    )
+
+
 def solution(mesh):
     return jax.shard_map(
-        on_device,
+        fused_device if fits(mesh) else on_device,
         mesh=mesh,
         in_specs=(
             P("dp", None),

time: 145 us -> 34.5 us (0.24)
  blocking collectives: 111 us -> 0 us
  Pallas kernels: 0 us -> 28.8 us
  starting transfers between devices: 10.7 us -> 0 us
  other arithmetic: 7.74 us -> 0 us
  waiting for transfers between devices: 7.67 us -> 0 us
  matrix products: 2.7 us -> 0 us
  local copies, waits for them, and re-layouts: 2.81 us -> 4.75 us
    all_gather x4 -> x0, blocking collectives: 45.7 us -> none  [the longest x1 30.4 us: on_device(): all_rows = lax.all_gather(attended_local, 'dp', axis=0, tiled=True)]
    unnamed x1 -> x0, blocking collectives: 36.5 us -> none
    pallas_call x0 -> x1, Pallas kernels: none -> 28.8 us  [fused_device(): pl.pallas_call(functools.partial(fused_kernel, dp, mp), out_shape=(jax.Sh...]
    psum x2 -> x0, blocking collectives: 21.5 us -> none  [the longest x1 11.2 us: on_device(): partial_cols = lax.psum(partial_cols, 'mp')]
    all_to_all x2 -> x0, starting transfers between devices: 10.7 us -> none  [the longest x1 7.31 us: on_device(): lax.all_to_all(normed, 'dp', split_axis=1, concat_axis=0, tiled=True)]
    all_to_all x2 -> x0, waiting for transfers between devices: 7.67 us -> none  [the longest x1 6.01 us: on_device(): lax.all_to_all(partial_cols, 'dp', split_axis=0, concat_axis=1, tiled=True)]
    pmax x1 -> x0, blocking collectives: 7.24 us -> none  [on_device(): global_peak = lax.pmax(peaks, 'mp')]
    unnamed x15 -> x8, local copies, waits for them, and re-layouts: 1.9 us -> 4.75 us
  transfers between devices with their start and end apart: 2 -> 0, of which waited for: 2 -> 0; matrix products, arithmetic and copies ran while one was open for 3% -> 0% of each run, Pallas kernels for 0% -> 0%
where the time goes in v1:
time: 34.5 us; the launch traced here: 34.2 us
  Pallas kernels  28.8 us (83%)
  local copies, waits for them, and re-layouts  4.75 us (14%)
  between operations  0.65 us (2%)
    pallas_call x1, Pallas kernels, fused_device(): pl.pallas_call(functools.partial(fused_kernel, dp, mp), out_shape=(jax.Sh...  28.8 us
    unnamed x8, local copies, waits for them, and re-layouts  4.75 us

profile of v1, /device:TPU:0, one launch (start us, length us, event | category | flops | bytes accessed | tf_op | source)
XLA Modules:
  0.0 34.2 jit_solution(4158146612072221880)
XLA Ops:
  0.6 2.1 %copy.14.out_hbm = bf16[1,512,576]{2,1,0:T(8,128)(2,1)} copy(bf16[1,512,576]{1,2,0:T(8,128)(2,1)} %param.17) | data formatting | bytes 1179648 | tf_op args[6]
  2.8 28.8 %shard_map.130 = (bf16[2,4608]{1,0:T(2,128)(2,1)}, bf16[1,2,8,128]{3,2,1,0:T(8,128)(2,1)}, bf16[1,2,8,128]{3,2,1,0:T(8,128)(2,1)}) custom-call(s32[2]{0:T(128)} %lengths_ref.1, s32[1,2]{1,0:T(1,128)} %windowed_ref.1, bf16[2,4608]{1,0:T(2,128)(2,1)} %hidden_ref.1, f32[1,4608]{1,0:T(1,128)} %in_gain_ref.1, f32[1,4608]{1,0:T(1,128)} %post_gain_ref.1, ...), custom_call_target="tpu_custom_call" | custom-call | tf_op jit(solution)/shard_map/pallas_call | solution.py:499
  31.6 0.0 copy-start.1
  31.6 1.3 %copy.18 = bf16[2,4608]{1,0:T(2,128)(2,1)} copy(bf16[2,4608]{1,0:T(2,128)(2,1)} %get-tuple-element.6) | data formatting | bytes 36864
  32.9 0.0 copy-done.1
  32.9 0.0 copy-start
  32.9 0.6 %copy.19 = bf16[1,2,8,128]{3,2,1,0:T(8,128)(2,1)} copy(bf16[1,2,8,128]{3,2,1,0:T(8,128)(2,1)S(1)} %copy-done.1) | data formatting | bytes 8192
  33.5 0.1 copy-done
  33.6 0.6 %copy.20 = bf16[1,2,8,128]{3,2,1,0:T(8,128)(2,1)} copy(bf16[1,2,8,128]{3,2,1,0:T(8,128)(2,1)S(1)} %copy-done) | data formatting | bytes 8192
Async XLA Ops:
  31.6 1.4 %copy-start.1 = (bf16[1,2,8,128]{3,2,1,0:T(8,128)(2,1)S(1)}, bf16[1,2,8,128]{3,2,1,0:T(8,128)(2,1)}, u32[]{:S(2)}) copy-start(bf16[1,2,8,128]{3,2,1,0:T(8,128)(2,1)} %get-tuple-element.7) | copy-start | bytes 12292
  32.9 0.7 %copy-start = (bf16[1,2,8,128]{3,2,1,0:T(8,128)(2,1)S(1)}, bf16[1,2,8,128]{3,2,1,0:T(8,128)(2,1)}, u32[]{:S(2)}) copy-start(bf16[1,2,8,128]{3,2,1,0:T(8,128)(2,1)} %get-tuple-element.8) | copy-start | bytes 12292

commit v2 on v1

--- a/solution.py
+++ b/solution.py
@@ -168,17 +168,38 @@
     query_heads = HEADS // parts
     key_heads = KV_HEADS // parts
     return (
-        HEADS % parts == 0
+        parts & (parts - 1) == 0
+        and mesh.shape["dp"] & (mesh.shape["dp"] - 1) == 0
+        and HEADS % parts == 0
         and KV_HEADS % parts == 0
         and query_heads == 2 * key_heads
         and query_heads + 2 * key_heads == BLOCK_ROWS
     )
+
+
+def low(index, size):
+    return index & (size - 1)
+
+
+def high(index, size):
+    return index >> (size.bit_length() - 1)
 
 
 def one_hot(rows, columns, match):
     row = lax.broadcasted_iota(jnp.int32, (rows, columns), 0)
     column = lax.broadcasted_iota(jnp.int32, (rows, columns), 1)
     return jnp.where(match(row, column), 1.0, 0.0).astype(jnp.bfloat16)
+
+
+def partners(mine, count):
+    found = []
+    for pattern in range(count):
+        there = 0
+        for bit in range(count.bit_length() - 1):
+            held = lax.rem(mine // 2**bit, 2)
+            there = there + 2**bit * (1 - held if pattern >> bit & 1 else held)
+        found.append(there)
+    return found
 
 
 def pick(selector, values):
@@ -231,8 +252,8 @@
     key_width = key_w.shape[1]
     query_heads = query_width // HEAD_DIM
     key_heads = key_width // HEAD_DIM
-    seq_block = key_cache_hbm.shape[2]
-    cache_rows = seq_block * KV_HEADS
+    cache_rows = key_cache_hbm.shape[2]
+    seq_block = cache_rows // KV_HEADS
     window_len = seq_block * mp // 2
 
     loads = [
@@ -248,13 +269,15 @@
             )
         )
     ]
+    peer_dp = partners(my_dp, dp)
+    peer_mp = partners(my_mp, mp)
+    others = [(i, j) for i in reversed(range(dp)) for j in reversed(range(mp)) if i + j > 0]
     barrier = pltpu.get_barrier_semaphore()
-    for step in range(1, devices):
-        there = lax.rem(me + step, devices)
+    for i, j in others:
         pl.semaphore_signal(
             barrier,
             inc=1,
-            device_id={"dp": there // mp, "mp": lax.rem(there, mp)},
+            device_id={"dp": peer_dp[i], "mp": peer_mp[j]},
             device_id_type=MESH_ID,
         )
     for load in loads:
@@ -268,8 +291,7 @@
     norm_recv[my_dp] = norm_send[my_dp]
 
     pl.semaphore_wait(barrier, devices - 1)
-    for step in range(1, dp):
-        there = lax.rem(my_dp + step, dp)
+    for there in reversed(peer_dp[1:]):
         pltpu.make_async_remote_copy(
             src_ref=norm_send.at[there],
             dst_ref=norm_recv.at[my_dp],
@@ -284,10 +306,9 @@
         pltpu.make_async_copy(block, block, sem).wait()
 
     def scatter(send, recv, stage, slot_of):
-        for step in range(1, devices):
-            there = lax.rem(me + step, devices)
-            there_dp = there // mp
-            there_mp = lax.rem(there, mp)
+        for i, j in others:
+            there_dp = peer_dp[i]
+            there_mp = peer_mp[j]
             pltpu.make_async_remote_copy(
                 src_ref=send.at[slot_of(there_dp, there_mp)],
                 dst_ref=recv.at[me],
@@ -329,7 +350,7 @@
         total_rows * BLOCK_ROWS,
         total_rows * BLOCK_ROWS,
         lambda row, column: column
-        == (row % BLOCK_ROWS) * total_rows + row // BLOCK_ROWS,
+        == low(row, BLOCK_ROWS) * total_rows + high(row, BLOCK_ROWS),
     )
     proj_send[...] = (
         pick(spread, stacked).astype(jnp.bfloat16).reshape(dp, rows * BLOCK_ROWS, HEAD_DIM)
@@ -341,11 +362,11 @@
     group_rows = mp * BLOCK_ROWS
     row = lax.broadcasted_iota(jnp.int32, (group_rows, cache_rows), 0)
     column = lax.broadcasted_iota(jnp.int32, (group_rows, cache_rows), 1)
-    in_block = row % BLOCK_ROWS
+    in_block = low(row, BLOCK_ROWS)
     head_match = (in_block < query_heads) & (
-        column % KV_HEADS == (row // BLOCK_ROWS) * key_heads + in_block // 2
-    )
-    position = my_mp * seq_block + column // KV_HEADS
+        low(column, KV_HEADS) == high(row, BLOCK_ROWS) * key_heads + high(in_block, 2)
+    )
+    position = my_mp * seq_block + high(column, KV_HEADS)
     allowed = []
     for r in range(rows):
         length = lengths_ref[r]
@@ -353,14 +374,14 @@
         allowed.append(head_match & (position < length) & (position > floor))
     self_row = lax.broadcasted_iota(jnp.int32, (group_rows, group_rows), 0)
     self_column = lax.broadcasted_iota(jnp.int32, (group_rows, group_rows), 1)
-    self_slot = self_row % BLOCK_ROWS
-    own_base = (self_row // BLOCK_ROWS) * BLOCK_ROWS + query_heads + self_slot // 2
+    self_slot = low(self_row, BLOCK_ROWS)
+    own_base = self_row - self_slot + query_heads + high(self_slot, 2)
     is_query = self_slot < query_heads
     self_key = is_query & (self_column == own_base)
     self_value = jnp.where(is_query & (self_column == own_base + key_heads), 1.0, 0.0).astype(
         jnp.bfloat16
     )
-    acc_row = lax.broadcasted_iota(jnp.int32, (group_rows, HEAD_DIM), 0) % BLOCK_ROWS
+    acc_row = low(lax.broadcasted_iota(jnp.int32, (group_rows, HEAD_DIM), 0), BLOCK_ROWS)
     self_share = jnp.where(my_mp == 0, 1.0, 0.0)
 
     finish(proj_recv, devices - 1, recv_sem.at[1])
@@ -381,13 +402,13 @@
         turned = turned.astype(jnp.bfloat16)
         rotated_rows.append(turned)
         raw_rows.append(raw)
-        flat_keys = keys[r].reshape(cache_rows, HEAD_DIM)
-        flat_values = values[r].reshape(cache_rows, HEAD_DIM)
+        flat_keys = keys[r]
+        flat_values = values[r]
         over_last = (((1,), (1,)), ((), ()))
         scores = lax.dot_general(
             queries, flat_keys, over_last, preferred_element_type=jnp.float32
         )
-        scores = SOFTCAP * jnp.tanh(scores / SOFTCAP)
+        scores = SOFTCAP * jnp.tanh(scores * (1.0 / SOFTCAP))
         exp_scores = jnp.where(allowed[r], jnp.exp(scores), 0.0)
         sums_exp = jnp.sum(exp_scores, axis=-1, keepdims=True)
         accumulated = jnp.dot(
@@ -395,7 +416,7 @@
         )
         own = lax.dot_general(queries, turned, over_last, preferred_element_type=jnp.float32)
         own = jnp.sum(jnp.where(self_key, own, 0.0), axis=-1, keepdims=True)
-        own = jnp.exp(SOFTCAP * jnp.tanh(own / SOFTCAP)) * self_share
+        own = jnp.exp(SOFTCAP * jnp.tanh(own * (1.0 / SOFTCAP))) * self_share
         accumulated = accumulated + own * pick(self_value, raw)
         sums_exp = jnp.broadcast_to(sums_exp + own, (group_rows, HEAD_DIM))
         message = jnp.where(
@@ -410,12 +431,12 @@
     raw_all = jnp.concatenate(raw_rows, axis=0)
 
     def owner(row, first):
-        head = row % KV_HEADS
+        head = low(row, KV_HEADS)
         return (
-            (row // KV_HEADS) * group_rows
-            + (head // key_heads) * BLOCK_ROWS
+            high(row, KV_HEADS) * group_rows
+            + high(head, key_heads) * BLOCK_ROWS
             + first
-            + head % key_heads
+            + low(head, key_heads)
         )
 
     key_rows = one_hot(
@@ -436,7 +457,7 @@
         query_heads * total_rows,
         total_rows * BLOCK_ROWS,
         lambda row, column: column
-        == (row % total_rows) * BLOCK_ROWS + row // total_rows,
+        == low(row, total_rows) * BLOCK_ROWS + high(row, total_rows),
     )
 
     loads[5].wait()
@@ -444,14 +465,16 @@
     mixed = jnp.sum(
         mix_recv[...].astype(jnp.float32).reshape(dp, mp, blocks, HEAD_DIM), axis=1
     ).reshape(dp * blocks, HEAD_DIM)
-    all_row = lax.broadcasted_iota(jnp.int32, mixed.shape, 0) % BLOCK_ROWS
+    all_row = low(lax.broadcasted_iota(jnp.int32, mixed.shape, 0), BLOCK_ROWS)
     weights = pltpu.roll(mixed, mixed.shape[0] - query_heads, 0)
     attended = jnp.where(all_row < query_heads, mixed / weights, 0.0).astype(jnp.bfloat16)
     heads = pick(gather, attended).astype(jnp.bfloat16)
     heads = jnp.concatenate(
         [heads[b * total_rows : (b + 1) * total_rows] for b in range(query_heads)], axis=1
     )
-    partial_cols = jnp.dot(heads, out_w[...], preferred_element_type=jnp.float32)
+    partial_cols = lax.dot_general(
+        heads, out_w[...], over_last, preferred_element_type=jnp.float32
+    )
     for part in range(dp):
         cols_send[part] = partial_cols[part * rows : (part + 1) * rows].astype(cols_send.dtype)
     scatter(cols_send, cols_recv, 3, lambda there_dp, there_mp: there_dp)
@@ -471,6 +494,12 @@
     finish(proj_recv, devices - 1, send_sem.at[1])
     finish(mix_recv, devices - 1, send_sem.at[2])
     finish(cols_recv, devices - 1, send_sem.at[3])
+
+
+def copy_kernel(a_ref, b_ref, c_ref, a_out, b_out, c_out):
+    a_out[...] = a_ref[...]
+    b_out[...] = b_ref[...]
+    c_out[...] = c_ref[...]
 
 
 def fused_device(
@@ -493,25 +522,27 @@
     out_slab = out_weight.shape[2]
     blocks = rows * BLOCK_ROWS
     half_word = jnp.bfloat16
+    flat = (LAYERS, rows, key_cache.shape[2] * KV_HEADS, HEAD_DIM)
+    out_shape = (
+        jax.ShapeDtypeStruct(hidden.shape, half_word),
+        jax.ShapeDtypeStruct((LAYERS, rows, KV_HEADS, HEAD_DIM), half_word),
+        jax.ShapeDtypeStruct((LAYERS, rows, KV_HEADS, HEAD_DIM), half_word),
+    )
     smem = pl.BlockSpec(memory_space=pltpu.SMEM)
     vmem = pl.BlockSpec(memory_space=pltpu.VMEM)
     far = pl.BlockSpec(memory_space=pl.ANY)
-    return pl.pallas_call(
+    results = pl.pallas_call(
         functools.partial(fused_kernel, dp, mp),
-        out_shape=(
-            jax.ShapeDtypeStruct(hidden.shape, half_word),
-            jax.ShapeDtypeStruct((LAYERS, rows, KV_HEADS, HEAD_DIM), half_word),
-            jax.ShapeDtypeStruct((LAYERS, rows, KV_HEADS, HEAD_DIM), half_word),
-        ),
+        out_shape=out_shape,
         in_specs=[smem, smem, vmem, vmem, vmem, far, far, far, far, far, far],
         out_specs=(vmem, vmem, vmem),
         scratch_shapes=[
             pltpu.VMEM(query_weight.shape[1:], half_word),
             pltpu.VMEM(key_weight.shape[1:], half_word),
             pltpu.VMEM(value_weight.shape[1:], half_word),
-            pltpu.VMEM(out_weight.shape[1:], half_word),
-            pltpu.VMEM(key_cache.shape[1:], half_word),
-            pltpu.VMEM(value_cache.shape[1:], half_word),
+            pltpu.VMEM((out_slab, out_weight.shape[1]), half_word),
+            pltpu.VMEM(flat[1:], half_word),
+            pltpu.VMEM(flat[1:], half_word),
             pltpu.VMEM((dp, rows, slab), half_word),
             pltpu.VMEM((dp, rows, slab), half_word),
             pltpu.VMEM((dp, blocks, HEAD_DIM), half_word),
@@ -534,10 +565,12 @@
         query_weight,
         key_weight,
         value_weight,
-        out_weight,
-        key_cache,
-        value_cache,
-    )
+        jnp.swapaxes(out_weight, 1, 2),
+        key_cache.reshape(flat),
+        value_cache.reshape(flat),
+    )
+    plain = pl.pallas_call(copy_kernel, out_shape=out_shape, in_specs=[vmem] * 3, out_specs=(vmem,) * 3)
+    return plain(*results)
 
 
 def solution(mesh):

time: 34.5 us -> 30.7 us (0.89)
  local copies, waits for them, and re-layouts: 4.75 us -> 0 us
  Pallas kernels: 28.8 us -> 29.9 us
    unnamed x8 -> x0, local copies, waits for them, and re-layouts: 4.75 us -> none
    pallas_call x1 -> x2, Pallas kernels: 28.8 us -> 29.9 us  [the longest x1 28.5 us: fused_device(): pl.pallas_call(functools.partial(fused_kernel, dp, mp), out_shape=out_sha...]
where the time goes in v2:
time: 30.7 us; the launch traced here: 30.5 us
  Pallas kernels  29.9 us (97%)
  between operations  0.64 us (2%)
    pallas_call x1, Pallas kernels, fused_device(): pl.pallas_call(functools.partial(fused_kernel, dp, mp), out_shape=out_sha...  28.5 us
    pallas_call x1, Pallas kernels, fused_device(): return plain(*results)  1.34 us

profile of v2, /device:TPU:0, one launch (start us, length us, event | category | flops | bytes accessed | tf_op | source)
XLA Modules:
  0.0 30.5 jit_solution(4118451186852424100)
XLA Ops:
  0.6 28.5 %shard_map.130 = (bf16[2,4608]{1,0:T(2,128)(2,1)}, bf16[1,2,8,128]{3,2,1,0:T(8,128)(2,1)}, bf16[1,2,8,128]{3,2,1,0:T(8,128)(2,1)}) custom-call(s32[2]{0:T(128)} %lengths_ref.1, s32[1,2]{1,0:T(1,128)} %windowed_ref.1, bf16[2,4608]{1,0:T(2,128)(2,1)} %hidden_ref.1, f32[1,4608]{1,0:T(1,128)} %in_gain_ref.1, f32[1,4608]{1,0:T(1,128)} %post_gain_ref.1, ...), custom_call_target="tpu_custom_call" | custom-call | tf_op jit(solution)/shard_map/pallas_call | solution.py:534
  29.2 1.3 %shard_map.131 = (bf16[2,4608]{1,0:T(2,128)(2,1)}, bf16[1,2,8,128]{3,2,1,0:T(8,128)(2,1)}, bf16[1,2,8,128]{3,2,1,0:T(8,128)(2,1)}) custom-call(bf16[2,4608]{1,0:T(2,128)(2,1)} %get-tuple-element.6.a_ref, bf16[1,2,8,128]{3,2,1,0:T(8,128)(2,1)} %get-tuple-element.7.b_ref, bf16[1,2,8,128]{3,2,1,0:T(8,128)(2,1)} %get-tuple-element.8.c_ref), custom_call_target="tpu_custom_call" | custom-call | tf_op jit(solution)/shard_map/pallas_call | solution.py:573

commit v3 on v2

--- a/solution.py
+++ b/solution.py
@@ -209,11 +209,11 @@
 def fused_kernel(
     dp,
     mp,
-    lengths_ref,
-    windowed_ref,
-    hidden_ref,
-    in_gain_ref,
-    post_gain_ref,
+    lengths_hbm,
+    windowed_hbm,
+    hidden_hbm,
+    in_gain_hbm,
+    post_gain_hbm,
     query_hbm,
     key_hbm,
     value_hbm,
@@ -223,6 +223,11 @@
     hidden_out_ref,
     new_keys_ref,
     new_values_ref,
+    lengths_ref,
+    windowed_ref,
+    hidden_ref,
+    in_gain_ref,
+    post_gain_ref,
     query_w,
     key_w,
     value_w,
@@ -233,8 +238,12 @@
     norm_recv,
     proj_send,
     proj_recv,
+    whole_send,
+    whole_recv,
     mix_send,
     mix_recv,
+    heads_send,
+    heads_recv,
     cols_send,
     cols_recv,
     load_sem,
@@ -260,12 +269,17 @@
         pltpu.make_async_copy(src, dst, load_sem.at[i])
         for i, (src, dst) in enumerate(
             (
+                (hidden_hbm, hidden_ref),
+                (in_gain_hbm, in_gain_ref),
+                (lengths_hbm, lengths_ref),
+                (windowed_hbm, windowed_ref),
                 (query_hbm.at[0], query_w),
                 (key_hbm.at[0], key_w),
                 (value_hbm.at[0], value_w),
                 (key_cache_hbm.at[0], keys),
                 (value_cache_hbm.at[0], values),
                 (out_hbm.at[0], out_w),
+                (post_gain_hbm, post_gain_ref),
             )
         )
     ]
@@ -273,7 +287,8 @@
     peer_mp = partners(my_mp, mp)
     others = [(i, j) for i in reversed(range(dp)) for j in reversed(range(mp)) if i + j > 0]
     barrier = pltpu.get_barrier_semaphore()
-    for i, j in others:
+    near = [(i, j) for i, j in others if i == 0 or j == 0]
+    for i, j in near:
         pl.semaphore_signal(
             barrier,
             inc=1,
@@ -282,42 +297,37 @@
         )
     for load in loads:
         load.start()
+    for load in loads[:2]:
+        load.wait()
 
     hidden = hidden_ref[...].astype(jnp.float32)
     mean_square = jnp.mean(hidden * hidden, axis=-1, keepdims=True)
     normed = hidden * lax.rsqrt(mean_square + EPSILON) * in_gain_ref[...]
     for part in range(dp):
         norm_send[part] = normed[:, part * slab : (part + 1) * slab].astype(jnp.bfloat16)
-    norm_recv[my_dp] = norm_send[my_dp]
-
-    pl.semaphore_wait(barrier, devices - 1)
-    for there in reversed(peer_dp[1:]):
-        pltpu.make_async_remote_copy(
-            src_ref=norm_send.at[there],
-            dst_ref=norm_recv.at[my_dp],
-            send_sem=send_sem.at[0],
-            recv_sem=recv_sem.at[0],
-            device_id={"dp": there, "mp": my_mp},
-            device_id_type=MESH_ID,
-        ).start()
-
+
+    pl.semaphore_wait(barrier, len(near))
     def finish(buffer, count, sem):
         block = buffer.at[pl.ds(0, count)]
         pltpu.make_async_copy(block, block, sem).wait()
 
-    def scatter(send, recv, stage, slot_of):
-        for i, j in others:
-            there_dp = peer_dp[i]
-            there_mp = peer_mp[j]
+    def exchange(recv, stage, targets, source, slot):
+        for i, j in targets:
             pltpu.make_async_remote_copy(
-                src_ref=send.at[slot_of(there_dp, there_mp)],
-                dst_ref=recv.at[me],
+                src_ref=source(peer_dp[i], peer_mp[j]),
+                dst_ref=recv.at[slot],
                 send_sem=send_sem.at[stage],
                 recv_sem=recv_sem.at[stage],
-                device_id={"dp": there_dp, "mp": there_mp},
+                device_id={"dp": peer_dp[i], "mp": peer_mp[j]},
                 device_id_type=MESH_ID,
             ).start()
-        recv[me] = send[slot_of(my_dp, my_mp)]
+
+    along_dp = [(i, j) for i, j in near if j == 0]
+    along_mp = [(i, j) for i, j in near if i == 0]
+    exchange(norm_recv, 0, along_dp, lambda a, b: norm_send.at[a], my_dp)
+    norm_recv[my_dp] = norm_send[my_dp]
+    for load in loads[2:4]:
+        load.wait()
 
     lane = lax.broadcasted_iota(jnp.int32, (BLOCK_ROWS, HEAD_DIM), 1)
     half = HEAD_DIM // 2
@@ -331,7 +341,7 @@
         sine = jnp.sin(angle)
         sines.append(jnp.where(lane < half, -sine, sine))
 
-    for load in loads[:3]:
+    for load in loads[4:7]:
         load.wait()
     finish(norm_recv, dp - 1, recv_sem.at[0])
     tokens = jnp.concatenate(
@@ -355,9 +365,10 @@
     proj_send[...] = (
         pick(spread, stacked).astype(jnp.bfloat16).reshape(dp, rows * BLOCK_ROWS, HEAD_DIM)
     )
-    scatter(proj_send, proj_recv, 1, lambda there_dp, there_mp: there_dp)
-
-    for load in loads[3:5]:
+    exchange(proj_recv, 1, along_dp, lambda a, b: proj_send.at[a], my_dp)
+    proj_recv[my_dp] = proj_send[my_dp]
+
+    for load in loads[7:9]:
         load.wait()
     group_rows = mp * BLOCK_ROWS
     row = lax.broadcasted_iota(jnp.int32, (group_rows, cache_rows), 0)
@@ -384,11 +395,13 @@
     acc_row = low(lax.broadcasted_iota(jnp.int32, (group_rows, HEAD_DIM), 0), BLOCK_ROWS)
     self_share = jnp.where(my_mp == 0, 1.0, 0.0)
 
-    finish(proj_recv, devices - 1, recv_sem.at[1])
+    finish(proj_recv, dp - 1, recv_sem.at[1])
     blocks = rows * BLOCK_ROWS
-    summed = jnp.sum(
-        proj_recv[...].astype(jnp.float32).reshape(dp, mp, blocks, HEAD_DIM), axis=0
-    )
+    whole_send[...] = jnp.sum(proj_recv[...].astype(jnp.float32), axis=0).astype(jnp.bfloat16)
+    exchange(whole_recv, 2, along_mp, lambda a, b: whole_send, my_mp)
+    whole_recv[my_mp] = whole_send[...]
+    finish(whole_recv, mp - 1, recv_sem.at[2])
+    summed = whole_recv[...].astype(jnp.float32)
     rotated_rows = []
     raw_rows = []
     for r in range(rows):
@@ -425,8 +438,20 @@
         mix_send[:, r * BLOCK_ROWS : (r + 1) * BLOCK_ROWS, :] = message.reshape(
             mp, BLOCK_ROWS, HEAD_DIM
         ).astype(mix_send.dtype)
-    scatter(mix_send, mix_recv, 2, lambda there_dp, there_mp: there_mp)
-
+    exchange(mix_recv, 3, along_mp, lambda a, b: mix_send.at[b], my_mp)
+    mix_recv[my_mp] = mix_send[my_mp]
+
+    finish(mix_recv, mp - 1, recv_sem.at[3])
+    mixed = jnp.sum(mix_recv[...].astype(jnp.float32), axis=0)
+    attended = []
+    for r in range(rows):
+        at = r * BLOCK_ROWS
+        attended.append(
+            mixed[at : at + query_heads] / mixed[at + query_heads : at + 2 * query_heads]
+        )
+    heads_send[...] = jnp.concatenate(attended, axis=0).astype(jnp.bfloat16)
+    exchange(heads_recv, 4, along_dp, lambda a, b: heads_send, my_dp)
+    heads_recv[my_dp] = heads_send[...]
     turned_all = jnp.concatenate(rotated_rows, axis=0)
     raw_all = jnp.concatenate(raw_rows, axis=0)
 
@@ -455,20 +480,15 @@
     )
     gather = one_hot(
         query_heads * total_rows,
-        total_rows * BLOCK_ROWS,
+        query_heads * total_rows,
         lambda row, column: column
-        == low(row, total_rows) * BLOCK_ROWS + high(row, total_rows),
-    )
-
-    loads[5].wait()
-    finish(mix_recv, devices - 1, recv_sem.at[2])
-    mixed = jnp.sum(
-        mix_recv[...].astype(jnp.float32).reshape(dp, mp, blocks, HEAD_DIM), axis=1
-    ).reshape(dp * blocks, HEAD_DIM)
-    all_row = low(lax.broadcasted_iota(jnp.int32, mixed.shape, 0), BLOCK_ROWS)
-    weights = pltpu.roll(mixed, mixed.shape[0] - query_heads, 0)
-    attended = jnp.where(all_row < query_heads, mixed / weights, 0.0).astype(jnp.bfloat16)
-    heads = pick(gather, attended).astype(jnp.bfloat16)
+        == low(row, total_rows) * query_heads + high(row, total_rows),
+    )
+    for load in loads[9:]:
+        load.wait()
+    finish(heads_recv, dp - 1, recv_sem.at[4])
+    attended = heads_recv[...].astype(jnp.float32).reshape(total_rows * query_heads, HEAD_DIM)
+    heads = pick(gather, attended.astype(jnp.bfloat16)).astype(jnp.bfloat16)
     heads = jnp.concatenate(
         [heads[b * total_rows : (b + 1) * total_rows] for b in range(query_heads)], axis=1
     )
@@ -477,8 +497,9 @@
     )
     for part in range(dp):
         cols_send[part] = partial_cols[part * rows : (part + 1) * rows].astype(cols_send.dtype)
-    scatter(cols_send, cols_recv, 3, lambda there_dp, there_mp: there_dp)
-    finish(cols_recv, devices - 1, recv_sem.at[3])
+    exchange(cols_recv, 5, others, lambda a, b: cols_send.at[a], me)
+    cols_recv[me] = cols_send[my_dp]
+    finish(cols_recv, devices - 1, recv_sem.at[5])
     pieces = []
     for part in range(dp):
         piece = cols_recv[part * mp].astype(jnp.float32)
@@ -491,9 +512,11 @@
     hidden_out_ref[...] = (hidden_ref[...].astype(jnp.float32) + update).astype(jnp.bfloat16)
 
     finish(norm_recv, dp - 1, send_sem.at[0])
-    finish(proj_recv, devices - 1, send_sem.at[1])
-    finish(mix_recv, devices - 1, send_sem.at[2])
-    finish(cols_recv, devices - 1, send_sem.at[3])
+    finish(proj_recv, dp - 1, send_sem.at[1])
+    finish(whole_recv, mp - 1, send_sem.at[2])
+    finish(mix_recv, mp - 1, send_sem.at[3])
+    finish(heads_recv, dp - 1, send_sem.at[4])
+    finish(cols_recv, devices - 1, send_sem.at[5])
 
 
 def copy_kernel(a_ref, b_ref, c_ref, a_out, b_out, c_out):
@@ -528,15 +551,19 @@
         jax.ShapeDtypeStruct((LAYERS, rows, KV_HEADS, HEAD_DIM), half_word),
         jax.ShapeDtypeStruct((LAYERS, rows, KV_HEADS, HEAD_DIM), half_word),
     )
-    smem = pl.BlockSpec(memory_space=pltpu.SMEM)
     vmem = pl.BlockSpec(memory_space=pltpu.VMEM)
     far = pl.BlockSpec(memory_space=pl.ANY)
     results = pl.pallas_call(
         functools.partial(fused_kernel, dp, mp),
         out_shape=out_shape,
-        in_specs=[smem, smem, vmem, vmem, vmem, far, far, far, far, far, far],
+        in_specs=[far] * 11,
         out_specs=(vmem, vmem, vmem),
         scratch_shapes=[
+            pltpu.SMEM(lengths.shape, lengths.dtype),
+            pltpu.SMEM(windowed.shape, windowed.dtype),
+            pltpu.VMEM(hidden.shape, hidden.dtype),
+            pltpu.VMEM(in_gain.shape, in_gain.dtype),
+            pltpu.VMEM(post_gain.shape, post_gain.dtype),
             pltpu.VMEM(query_weight.shape[1:], half_word),
             pltpu.VMEM(key_weight.shape[1:], half_word),
             pltpu.VMEM(value_weight.shape[1:], half_word),
@@ -546,14 +573,18 @@
             pltpu.VMEM((dp, rows, slab), half_word),
             pltpu.VMEM((dp, rows, slab), half_word),
             pltpu.VMEM((dp, blocks, HEAD_DIM), half_word),
-            pltpu.VMEM((dp * mp, blocks, HEAD_DIM), half_word),
+            pltpu.VMEM((dp, blocks, HEAD_DIM), half_word),
+            pltpu.VMEM((blocks, HEAD_DIM), half_word),
             pltpu.VMEM((mp, blocks, HEAD_DIM), half_word),
-            pltpu.VMEM((dp * mp, blocks, HEAD_DIM), half_word),
+            pltpu.VMEM((mp, blocks, HEAD_DIM), half_word),
+            pltpu.VMEM((mp, blocks, HEAD_DIM), half_word),
+            pltpu.VMEM((rows * out_weight.shape[1] // HEAD_DIM, HEAD_DIM), half_word),
+            pltpu.VMEM((dp, rows * out_weight.shape[1] // HEAD_DIM, HEAD_DIM), half_word),
             pltpu.VMEM((dp, rows, out_slab), half_word),
             pltpu.VMEM((dp * mp, rows, out_slab), half_word),
+            pltpu.SemaphoreType.DMA((11,)),
             pltpu.SemaphoreType.DMA((6,)),
-            pltpu.SemaphoreType.DMA((4,)),
-            pltpu.SemaphoreType.DMA((4,)),
+            pltpu.SemaphoreType.DMA((6,)),
         ],
         compiler_params=pltpu.CompilerParams(collective_id=0, has_side_effects=True),
     )(

time: 30.7 us -> 32.7 us (1.065)
  Pallas kernels: 29.9 us -> 31.9 us
    pallas_call x1, Pallas kernels: 28.5 us -> 30.5 us  [fused_device(): pl.pallas_call(functools.partial(fused_kernel, dp, mp), out_shape=out_sha...]
where the time goes in v3:
time: 32.7 us; the launch traced here: 32.5 us
  Pallas kernels  31.9 us (98%)
  between operations  0.64 us (2%)
    pallas_call x1, Pallas kernels, fused_device(): pl.pallas_call(functools.partial(fused_kernel, dp, mp), out_shape=out_sha...  30.5 us
    pallas_call x1, Pallas kernels, fused_device(): return plain(*results)  1.34 us

profile of v3, /device:TPU:0, one launch (start us, length us, event | category | flops | bytes accessed | tf_op | source)
XLA Modules:
  0.0 32.5 jit_solution(1783965472073583912)
XLA Ops:
  0.6 30.5 %shard_map.130 = (bf16[2,4608]{1,0:T(2,128)(2,1)}, bf16[1,2,8,128]{3,2,1,0:T(8,128)(2,1)}, bf16[1,2,8,128]{3,2,1,0:T(8,128)(2,1)}) custom-call(s32[2]{0:T(128)} %lengths_hbm.1, s32[1,2]{1,0:T(1,128)} %windowed_hbm.1, bf16[2,4608]{1,0:T(2,128)(2,1)} %hidden_hbm.1, f32[1,4608]{1,0:T(1,128)} %in_gain_hbm.1, f32[1,4608]{1,0:T(1,128)} %post_gain_hbm.1, ...), custom_call_target="tpu_custom_call" | custom-call | tf_op jit(solution)/shard_map/pallas_call | solution.py:556
  31.2 1.3 %shard_map.131 = (bf16[2,4608]{1,0:T(2,128)(2,1)}, bf16[1,2,8,128]{3,2,1,0:T(8,128)(2,1)}, bf16[1,2,8,128]{3,2,1,0:T(8,128)(2,1)}) custom-call(bf16[2,4608]{1,0:T(2,128)(2,1)} %get-tuple-element.6.a_ref, bf16[1,2,8,128]{3,2,1,0:T(8,128)(2,1)} %get-tuple-element.7.b_ref, bf16[1,2,8,128]{3,2,1,0:T(8,128)(2,1)} %get-tuple-element.8.c_ref), custom_call_target="tpu_custom_call" | custom-call | tf_op jit(solution)/shard_map/pallas_call | solution.py:604

commit v4 on v3

--- a/solution.py
+++ b/solution.py
@@ -160,20 +160,17 @@
 
 
 MESH_ID = pl.DeviceIdType.MESH
-BLOCK_ROWS = 8
-
-
-def fits(mesh):
-    parts = mesh.shape["mp"]
-    query_heads = HEADS // parts
-    key_heads = KV_HEADS // parts
+TILE_ROWS = 8
+
+
+def fits(rows, dp, mp):
     return (
-        parts & (parts - 1) == 0
-        and mesh.shape["dp"] & (mesh.shape["dp"] - 1) == 0
-        and HEADS % parts == 0
-        and KV_HEADS % parts == 0
-        and query_heads == 2 * key_heads
-        and query_heads + 2 * key_heads == BLOCK_ROWS
+        mp & (mp - 1) == 0
+        and dp & (dp - 1) == 0
+        and HEADS % mp == 0
+        and KV_HEADS % mp == 0
+        and HEADS == 2 * KV_HEADS
+        and rows * HEADS // mp == TILE_ROWS
     )
 
 
@@ -236,14 +233,16 @@
     values,
     norm_send,
     norm_recv,
-    proj_send,
-    proj_recv,
-    whole_send,
-    whole_recv,
+    query_send,
+    query_recv,
+    pair_send,
+    pair_recv,
     mix_send,
     mix_recv,
-    heads_send,
-    heads_recv,
+    sums_send,
+    sums_recv,
+    token_send,
+    token_recv,
     cols_send,
     cols_recv,
     load_sem,
@@ -287,8 +286,7 @@
     peer_mp = partners(my_mp, mp)
     others = [(i, j) for i in reversed(range(dp)) for j in reversed(range(mp)) if i + j > 0]
     barrier = pltpu.get_barrier_semaphore()
-    near = [(i, j) for i, j in others if i == 0 or j == 0]
-    for i, j in near:
+    for i, j in others:
         pl.semaphore_signal(
             barrier,
             inc=1,
@@ -306,7 +304,7 @@
     for part in range(dp):
         norm_send[part] = normed[:, part * slab : (part + 1) * slab].astype(jnp.bfloat16)
 
-    pl.semaphore_wait(barrier, len(near))
+    pl.semaphore_wait(barrier, devices - 1)
     def finish(buffer, count, sem):
         block = buffer.at[pl.ds(0, count)]
         pltpu.make_async_copy(block, block, sem).wait()
@@ -322,24 +320,26 @@
                 device_id_type=MESH_ID,
             ).start()
 
-    along_dp = [(i, j) for i, j in near if j == 0]
-    along_mp = [(i, j) for i, j in near if i == 0]
+    along_dp = [(i, j) for i, j in others if j == 0]
+    along_mp = [(i, j) for i, j in others if i == 0]
     exchange(norm_recv, 0, along_dp, lambda a, b: norm_send.at[a], my_dp)
     norm_recv[my_dp] = norm_send[my_dp]
     for load in loads[2:4]:
         load.wait()
 
-    lane = lax.broadcasted_iota(jnp.int32, (BLOCK_ROWS, HEAD_DIM), 1)
+    block = rows * query_heads
     half = HEAD_DIM // 2
-    pair = jnp.where(lane < half, lane, lane - half).astype(jnp.float32)
+    lane = lax.broadcasted_iota(jnp.int32, (block, HEAD_DIM), 1)
+    request = high(lax.broadcasted_iota(jnp.int32, (block, HEAD_DIM), 0), query_heads)
+    pair = low(lane, half).astype(jnp.float32)
     frequency = jnp.exp(pair * (-2.0 / HEAD_DIM * math.log(ROPE_BASE)))
-    cosines = []
-    sines = []
-    for r in range(rows):
-        angle = lengths_ref[r].astype(jnp.float32) * frequency
-        cosines.append(jnp.cos(angle))
-        sine = jnp.sin(angle)
-        sines.append(jnp.where(lane < half, -sine, sine))
+    place = jnp.full((block, HEAD_DIM), lengths_ref[0], jnp.int32)
+    for r in range(1, rows):
+        place = jnp.where(request == r, lengths_ref[r], place)
+    angle = place.astype(jnp.float32) * frequency
+    cosine = jnp.cos(angle)
+    sine = jnp.sin(angle)
+    sine = jnp.where(lane < half, -sine, sine)
 
     for load in loads[4:7]:
         load.wait()
@@ -347,137 +347,102 @@
     tokens = jnp.concatenate(
         [norm_recv[part].astype(jnp.float32) for part in range(dp)], axis=0
     ).astype(jnp.bfloat16)
-    parts = [
-        jnp.dot(tokens, weight[...], preferred_element_type=jnp.float32)
-        for weight in (query_w, key_w, value_w)
-    ]
-    pieces = []
-    for part in parts:
-        for at in range(0, part.shape[1], HEAD_DIM):
-            pieces.append(part[:, at : at + HEAD_DIM])
-    stacked = jnp.concatenate(pieces, axis=0).astype(jnp.bfloat16)
     spread = one_hot(
-        total_rows * BLOCK_ROWS,
-        total_rows * BLOCK_ROWS,
+        total_rows * query_heads,
+        total_rows * query_heads,
         lambda row, column: column
-        == low(row, BLOCK_ROWS) * total_rows + high(row, BLOCK_ROWS),
-    )
-    proj_send[...] = (
-        pick(spread, stacked).astype(jnp.bfloat16).reshape(dp, rows * BLOCK_ROWS, HEAD_DIM)
-    )
-    exchange(proj_recv, 1, along_dp, lambda a, b: proj_send.at[a], my_dp)
-    proj_recv[my_dp] = proj_send[my_dp]
+        == low(row, query_heads) * total_rows + high(row, query_heads),
+    )
+
+    def by_owner(parts):
+        pieces = [
+            part[:, at : at + HEAD_DIM]
+            for part in parts
+            for at in range(0, part.shape[1], HEAD_DIM)
+        ]
+        stacked = jnp.concatenate(pieces, axis=0).astype(jnp.bfloat16)
+        return pick(spread, stacked).astype(jnp.bfloat16).reshape(dp, block, HEAD_DIM)
+
+    query_send[...] = by_owner([pick(tokens, query_w[...])])
+    exchange(query_recv, 1, others, lambda a, b: query_send.at[a], me)
+    query_recv[me] = query_send[my_dp]
+    pair_send[...] = by_owner([pick(tokens, key_w[...]), pick(tokens, value_w[...])])
+    exchange(pair_recv, 2, along_dp, lambda a, b: pair_send.at[a], my_dp)
+    pair_recv[my_dp] = pair_send[my_dp]
 
     for load in loads[7:9]:
         load.wait()
-    group_rows = mp * BLOCK_ROWS
+    group_rows = mp * block
     row = lax.broadcasted_iota(jnp.int32, (group_rows, cache_rows), 0)
     column = lax.broadcasted_iota(jnp.int32, (group_rows, cache_rows), 1)
-    in_block = low(row, BLOCK_ROWS)
-    head_match = (in_block < query_heads) & (
-        low(column, KV_HEADS) == high(row, BLOCK_ROWS) * key_heads + high(in_block, 2)
-    )
+    head_match = low(column, KV_HEADS) == high(row, block) * key_heads + high(
+        low(row, query_heads), 2
+    )
+    row_request = high(low(row, block), query_heads)
     position = my_mp * seq_block + high(column, KV_HEADS)
     allowed = []
     for r in range(rows):
         length = lengths_ref[r]
         floor = jnp.where(windowed_ref[0, r] == 0, -1, length - window_len)
-        allowed.append(head_match & (position < length) & (position > floor))
-    self_row = lax.broadcasted_iota(jnp.int32, (group_rows, group_rows), 0)
-    self_column = lax.broadcasted_iota(jnp.int32, (group_rows, group_rows), 1)
-    self_slot = low(self_row, BLOCK_ROWS)
-    own_base = self_row - self_slot + query_heads + high(self_slot, 2)
-    is_query = self_slot < query_heads
-    self_key = is_query & (self_column == own_base)
-    self_value = jnp.where(is_query & (self_column == own_base + key_heads), 1.0, 0.0).astype(
-        jnp.bfloat16
-    )
-    acc_row = low(lax.broadcasted_iota(jnp.int32, (group_rows, HEAD_DIM), 0), BLOCK_ROWS)
-    self_share = jnp.where(my_mp == 0, 1.0, 0.0)
-
-    finish(proj_recv, dp - 1, recv_sem.at[1])
-    blocks = rows * BLOCK_ROWS
-    whole_send[...] = jnp.sum(proj_recv[...].astype(jnp.float32), axis=0).astype(jnp.bfloat16)
-    exchange(whole_recv, 2, along_mp, lambda a, b: whole_send, my_mp)
-    whole_recv[my_mp] = whole_send[...]
-    finish(whole_recv, mp - 1, recv_sem.at[2])
-    summed = whole_recv[...].astype(jnp.float32)
-    rotated_rows = []
-    raw_rows = []
+        allowed.append(
+            head_match & (row_request == r) & (position < length) & (position > floor)
+        )
+    own_row = lax.broadcasted_iota(jnp.int32, (group_rows, block), 0)
+    own_column = lax.broadcasted_iota(jnp.int32, (group_rows, block), 1)
+    own_base = low(own_row, block) - low(own_row, query_heads) + high(low(own_row, query_heads), 2)
+    own_group = high(own_row, block) == my_mp
+    own_key = own_group & (own_column == own_base)
+    own_value = jnp.where(own_column == own_base + key_heads, 1.0, 0.0).astype(jnp.bfloat16)
+    group_lane = lax.broadcasted_iota(jnp.int32, (group_rows, HEAD_DIM), 1)
+    group_row = low(lax.broadcasted_iota(jnp.int32, (group_rows, HEAD_DIM), 0), block)
+    over_last = (((1,), (1,)), ((), ()))
+
+    def turn(raw):
+        return raw * cosine + pltpu.roll(raw, half, raw.ndim - 1) * sine
+
+    finish(query_recv, devices - 1, recv_sem.at[1])
+    raw = jnp.sum(
+        query_recv[...].astype(jnp.float32).reshape(dp, mp, block, HEAD_DIM), axis=0
+    )
+    raw = raw.astype(jnp.bfloat16).astype(jnp.float32)
+    queries = jnp.concatenate([turn(raw[m]) for m in range(mp)], axis=0)
+    queries = (queries * HEAD_DIM ** (-0.5)).astype(jnp.bfloat16)
+    accumulated = jnp.zeros((group_rows, HEAD_DIM), jnp.float32)
+    sums_exp = jnp.zeros((group_rows, 1), jnp.float32)
     for r in range(rows):
-        raw = summed[:, r * BLOCK_ROWS : (r + 1) * BLOCK_ROWS, :].reshape(group_rows, HEAD_DIM)
-        raw = raw.astype(jnp.bfloat16)
-        wide = raw.astype(jnp.float32)
-        cosine = jnp.concatenate([cosines[r]] * mp, axis=0)
-        sine = jnp.concatenate([sines[r]] * mp, axis=0)
-        turned = wide * cosine + pltpu.roll(wide, half, 1) * sine
-        queries = (turned * HEAD_DIM ** (-0.5)).astype(jnp.bfloat16)
-        turned = turned.astype(jnp.bfloat16)
-        rotated_rows.append(turned)
-        raw_rows.append(raw)
-        flat_keys = keys[r]
-        flat_values = values[r]
-        over_last = (((1,), (1,)), ((), ()))
         scores = lax.dot_general(
-            queries, flat_keys, over_last, preferred_element_type=jnp.float32
+            queries, keys[r], over_last, preferred_element_type=jnp.float32
         )
         scores = SOFTCAP * jnp.tanh(scores * (1.0 / SOFTCAP))
         exp_scores = jnp.where(allowed[r], jnp.exp(scores), 0.0)
-        sums_exp = jnp.sum(exp_scores, axis=-1, keepdims=True)
-        accumulated = jnp.dot(
-            exp_scores.astype(jnp.bfloat16), flat_values, preferred_element_type=jnp.float32
-        )
-        own = lax.dot_general(queries, turned, over_last, preferred_element_type=jnp.float32)
-        own = jnp.sum(jnp.where(self_key, own, 0.0), axis=-1, keepdims=True)
-        own = jnp.exp(SOFTCAP * jnp.tanh(own * (1.0 / SOFTCAP))) * self_share
-        accumulated = accumulated + own * pick(self_value, raw)
-        sums_exp = jnp.broadcast_to(sums_exp + own, (group_rows, HEAD_DIM))
-        message = jnp.where(
-            acc_row < query_heads, accumulated, pltpu.roll(sums_exp, query_heads, 0)
-        )
-        mix_send[:, r * BLOCK_ROWS : (r + 1) * BLOCK_ROWS, :] = message.reshape(
-            mp, BLOCK_ROWS, HEAD_DIM
-        ).astype(mix_send.dtype)
-    exchange(mix_recv, 3, along_mp, lambda a, b: mix_send.at[b], my_mp)
-    mix_recv[my_mp] = mix_send[my_mp]
-
-    finish(mix_recv, mp - 1, recv_sem.at[3])
-    mixed = jnp.sum(mix_recv[...].astype(jnp.float32), axis=0)
-    attended = []
-    for r in range(rows):
-        at = r * BLOCK_ROWS
-        attended.append(
-            mixed[at : at + query_heads] / mixed[at + query_heads : at + 2 * query_heads]
-        )
-    heads_send[...] = jnp.concatenate(attended, axis=0).astype(jnp.bfloat16)
-    exchange(heads_recv, 4, along_dp, lambda a, b: heads_send, my_dp)
-    heads_recv[my_dp] = heads_send[...]
-    turned_all = jnp.concatenate(rotated_rows, axis=0)
-    raw_all = jnp.concatenate(raw_rows, axis=0)
-
-    def owner(row, first):
-        head = low(row, KV_HEADS)
-        return (
-            high(row, KV_HEADS) * group_rows
-            + high(head, key_heads) * BLOCK_ROWS
-            + first
-            + low(head, key_heads)
-        )
-
-    key_rows = one_hot(
-        rows * KV_HEADS, rows * group_rows, lambda row, column: column == owner(row, query_heads)
-    )
-    value_rows = one_hot(
-        rows * KV_HEADS,
-        rows * group_rows,
-        lambda row, column: column == owner(row, query_heads + key_heads),
-    )
-    new_keys_ref[...] = (
-        pick(key_rows, turned_all).astype(jnp.bfloat16).reshape(new_keys_ref.shape)
-    )
-    new_values_ref[...] = (
-        pick(value_rows, raw_all).astype(jnp.bfloat16).reshape(new_values_ref.shape)
-    )
+        sums_exp = sums_exp + jnp.sum(exp_scores, axis=-1, keepdims=True)
+        accumulated = accumulated + pick(exp_scores.astype(jnp.bfloat16), values[r])
+
+    finish(pair_recv, dp - 1, recv_sem.at[2])
+    pair_raw = jnp.sum(pair_recv[...].astype(jnp.float32), axis=0).astype(jnp.bfloat16)
+    pair_wide = pair_raw.astype(jnp.float32)
+    token = turn(pair_wide).astype(jnp.bfloat16)
+    own = lax.dot_general(queries, token, over_last, preferred_element_type=jnp.float32)
+    own = jnp.sum(jnp.where(own_key, own, 0.0), axis=-1, keepdims=True)
+    own = jnp.exp(SOFTCAP * jnp.tanh(own * (1.0 / SOFTCAP)))
+    own = jnp.where(own_group[:, :1], own, 0.0)
+    accumulated = accumulated + own * pick(own_value, pair_raw)
+    sums_exp = sums_exp + own
+    mix_send[...] = accumulated.reshape(mp, block, HEAD_DIM).astype(mix_send.dtype)
+    sums_send[...] = jnp.sum(
+        jnp.where(group_lane == group_row, sums_exp, 0.0).reshape(mp, block, HEAD_DIM),
+        axis=1,
+        keepdims=True,
+    )
+    exchange(mix_recv, 3, others, lambda a, b: mix_send.at[b], me)
+    exchange(sums_recv, 4, others, lambda a, b: sums_send.at[b], me)
+    mix_recv[me] = mix_send[my_mp]
+    sums_recv[me] = sums_send[my_mp]
+    is_key = low(lax.broadcasted_iota(jnp.int32, (block, HEAD_DIM), 0), query_heads) < key_heads
+    token_send[...] = jnp.where(is_key, token.astype(jnp.float32), pair_wide).astype(jnp.bfloat16)
+    exchange(token_recv, 5, along_mp, lambda a, b: token_send, my_mp)
+    token_recv[my_mp] = token_send[...]
+
     gather = one_hot(
         query_heads * total_rows,
         query_heads * total_rows,
@@ -486,9 +451,17 @@
     )
     for load in loads[9:]:
         load.wait()
-    finish(heads_recv, dp - 1, recv_sem.at[4])
-    attended = heads_recv[...].astype(jnp.float32).reshape(total_rows * query_heads, HEAD_DIM)
-    heads = pick(gather, attended.astype(jnp.bfloat16)).astype(jnp.bfloat16)
+    finish(mix_recv, devices - 1, recv_sem.at[3])
+    mixed = jnp.sum(
+        mix_recv[...].astype(jnp.float32).reshape(dp, mp, block, HEAD_DIM), axis=1
+    )
+    finish(sums_recv, devices - 1, recv_sem.at[4])
+    sums = jnp.sum(sums_recv[...].reshape(dp, mp, 1, HEAD_DIM), axis=1)
+    at_row = lax.broadcasted_iota(jnp.int32, mixed.shape, 1)
+    at_lane = lax.broadcasted_iota(jnp.int32, mixed.shape, 2)
+    sums = jnp.sum(jnp.where(at_row == at_lane, sums, 0.0), axis=-1, keepdims=True)
+    attended = (mixed / sums).reshape(dp * block, HEAD_DIM).astype(jnp.bfloat16)
+    heads = pick(gather, attended).astype(jnp.bfloat16)
     heads = jnp.concatenate(
         [heads[b * total_rows : (b + 1) * total_rows] for b in range(query_heads)], axis=1
     )
@@ -497,9 +470,27 @@
     )
     for part in range(dp):
         cols_send[part] = partial_cols[part * rows : (part + 1) * rows].astype(cols_send.dtype)
-    exchange(cols_recv, 5, others, lambda a, b: cols_send.at[a], me)
+    exchange(cols_recv, 6, others, lambda a, b: cols_send.at[a], me)
     cols_recv[me] = cols_send[my_dp]
-    finish(cols_recv, devices - 1, recv_sem.at[5])
+
+    def owner(row, first):
+        head = low(row, KV_HEADS)
+        return (
+            high(head, key_heads) * block
+            + high(row, KV_HEADS) * query_heads
+            + first
+            + low(head, key_heads)
+        )
+
+    finish(token_recv, mp - 1, recv_sem.at[5])
+    tokens_new = token_recv[...].astype(jnp.float32).reshape(group_rows, HEAD_DIM)
+    tokens_new = tokens_new.astype(jnp.bfloat16)
+    for first, out_ref in ((0, new_keys_ref), (key_heads, new_values_ref)):
+        chosen = one_hot(
+            rows * KV_HEADS, group_rows, lambda row, column: column == owner(row, first)
+        )
+        out_ref[...] = pick(chosen, tokens_new).astype(jnp.bfloat16).reshape(out_ref.shape)
+    finish(cols_recv, devices - 1, recv_sem.at[6])
     pieces = []
     for part in range(dp):
         piece = cols_recv[part * mp].astype(jnp.float32)
@@ -512,11 +503,12 @@
     hidden_out_ref[...] = (hidden_ref[...].astype(jnp.float32) + update).astype(jnp.bfloat16)
 
     finish(norm_recv, dp - 1, send_sem.at[0])
-    finish(proj_recv, dp - 1, send_sem.at[1])
-    finish(whole_recv, mp - 1, send_sem.at[2])
-    finish(mix_recv, mp - 1, send_sem.at[3])
-    finish(heads_recv, dp - 1, send_sem.at[4])
-    finish(cols_recv, devices - 1, send_sem.at[5])
+    finish(query_recv, devices - 1, send_sem.at[1])
+    finish(pair_recv, dp - 1, send_sem.at[2])
+    finish(mix_recv, devices - 1, send_sem.at[3])
+    finish(sums_recv, devices - 1, send_sem.at[4])
+    finish(token_recv, mp - 1, send_sem.at[5])
+    finish(cols_recv, devices - 1, send_sem.at[6])
 
 
 def copy_kernel(a_ref, b_ref, c_ref, a_out, b_out, c_out):
@@ -543,7 +535,7 @@
     rows = hidden.shape[0]
     slab = query_weight.shape[1]
     out_slab = out_weight.shape[2]
-    blocks = rows * BLOCK_ROWS
+    block = rows * query_weight.shape[2] // HEAD_DIM
     half_word = jnp.bfloat16
     flat = (LAYERS, rows, key_cache.shape[2] * KV_HEADS, HEAD_DIM)
     out_shape = (
@@ -572,19 +564,21 @@
             pltpu.VMEM(flat[1:], half_word),
             pltpu.VMEM((dp, rows, slab), half_word),
             pltpu.VMEM((dp, rows, slab), half_word),
-            pltpu.VMEM((dp, blocks, HEAD_DIM), half_word),
-            pltpu.VMEM((dp, blocks, HEAD_DIM), half_word),
-            pltpu.VMEM((blocks, HEAD_DIM), half_word),
-            pltpu.VMEM((mp, blocks, HEAD_DIM), half_word),
-            pltpu.VMEM((mp, blocks, HEAD_DIM), half_word),
-            pltpu.VMEM((mp, blocks, HEAD_DIM), half_word),
-            pltpu.VMEM((rows * out_weight.shape[1] // HEAD_DIM, HEAD_DIM), half_word),
-            pltpu.VMEM((dp, rows * out_weight.shape[1] // HEAD_DIM, HEAD_DIM), half_word),
+            pltpu.VMEM((dp, block, HEAD_DIM), half_word),
+            pltpu.VMEM((dp * mp, block, HEAD_DIM), half_word),
+            pltpu.VMEM((dp, block, HEAD_DIM), half_word),
+            pltpu.VMEM((dp, block, HEAD_DIM), half_word),
+            pltpu.VMEM((mp, block, HEAD_DIM), half_word),
+            pltpu.VMEM((dp * mp, block, HEAD_DIM), half_word),
+            pltpu.VMEM((mp, 1, HEAD_DIM), jnp.float32),
+            pltpu.VMEM((dp * mp, 1, HEAD_DIM), jnp.float32),
+            pltpu.VMEM((block, HEAD_DIM), half_word),
+            pltpu.VMEM((mp, block, HEAD_DIM), half_word),
             pltpu.VMEM((dp, rows, out_slab), half_word),
             pltpu.VMEM((dp * mp, rows, out_slab), half_word),
             pltpu.SemaphoreType.DMA((11,)),
-            pltpu.SemaphoreType.DMA((6,)),
-            pltpu.SemaphoreType.DMA((6,)),
+            pltpu.SemaphoreType.DMA((7,)),
+            pltpu.SemaphoreType.DMA((7,)),
         ],
         compiler_params=pltpu.CompilerParams(collective_id=0, has_side_effects=True),
     )(
@@ -604,9 +598,14 @@
     return plain(*results)
 
 
+def device_step(hidden, *rest):
+    fused = fits(hidden.shape[0], lax.axis_size("dp"), lax.axis_size("mp"))
+    return (fused_device if fused else on_device)(hidden, *rest)
+
+
 def solution(mesh):
     return jax.shard_map(
-        fused_device if fits(mesh) else on_device,
+        device_step,
         mesh=mesh,
         in_specs=(
             P("dp", None),

time: 32.7 us -> 29.4 us (0.90)
  Pallas kernels: 31.9 us -> 28.6 us
    pallas_call x1, Pallas kernels: 30.5 us -> 27.2 us  [fused_device(): pl.pallas_call(functools.partial(fused_kernel, dp, mp), out_shape=out_sha...]
where the time goes in v4:
time: 29.4 us; the launch traced here: 29.2 us
  Pallas kernels  28.6 us (97%)
  between operations  0.64 us (2%)
    pallas_call x1, Pallas kernels, fused_device(): pl.pallas_call(functools.partial(fused_kernel, dp, mp), out_shape=out_sha...  27.2 us
    pallas_call x1, Pallas kernels, fused_device(): return plain(*results)  1.34 us

profile of v4, /device:TPU:0, one launch (start us, length us, event | category | flops | bytes accessed | tf_op | source)
XLA Modules:
  0.0 29.2 jit_solution(1707074678007013284)
XLA Ops:
  0.6 27.2 %shard_map.130 = (bf16[2,4608]{1,0:T(2,128)(2,1)}, bf16[1,2,8,128]{3,2,1,0:T(8,128)(2,1)}, bf16[1,2,8,128]{3,2,1,0:T(8,128)(2,1)}) custom-call(s32[2]{0:T(128)} %lengths_hbm.1, s32[1,2]{1,0:T(1,128)} %windowed_hbm.1, bf16[2,4608]{1,0:T(2,128)(2,1)} %hidden_hbm.1, f32[1,4608]{1,0:T(1,128)} %in_gain_hbm.1, f32[1,4608]{1,0:T(1,128)} %post_gain_hbm.1, ...), custom_call_target="tpu_custom_call" | custom-call | tf_op jit(solution)/shard_map/pallas_call | solution.py:548
  27.9 1.3 %shard_map.131 = (bf16[2,4608]{1,0:T(2,128)(2,1)}, bf16[1,2,8,128]{3,2,1,0:T(8,128)(2,1)}, bf16[1,2,8,128]{3,2,1,0:T(8,128)(2,1)}) custom-call(bf16[2,4608]{1,0:T(2,128)(2,1)} %get-tuple-element.6.a_ref, bf16[1,2,8,128]{3,2,1,0:T(8,128)(2,1)} %get-tuple-element.7.b_ref, bf16[1,2,8,128]{3,2,1,0:T(8,128)(2,1)} %get-tuple-element.8.c_ref), custom_call_target="tpu_custom_call" | custom-call | tf_op jit(solution)/shard_map/pallas_call | solution.py:598

commit v5 on v4

--- a/solution.py
+++ b/solution.py
@@ -547,7 +547,7 @@
     far = pl.BlockSpec(memory_space=pl.ANY)
     results = pl.pallas_call(
         functools.partial(fused_kernel, dp, mp),
-        out_shape=out_shape,
+        out_shape=tuple(pltpu.VMEM(held.shape, held.dtype) for held in out_shape),
         in_specs=[far] * 11,
         out_specs=(vmem, vmem, vmem),
         scratch_shapes=[
@@ -595,7 +595,7 @@
         value_cache.reshape(flat),
     )
     plain = pl.pallas_call(copy_kernel, out_shape=out_shape, in_specs=[vmem] * 3, out_specs=(vmem,) * 3)
-    return plain(*results)
+    return plain(*(pltpu.with_memory_space_constraint(held, pltpu.VMEM) for held in results))
 
 
 def device_step(hidden, *rest):

time: 29.4 us -> 28 us (0.952)
  Pallas kernels: 28.6 us -> 27.2 us
    pallas_call x2, Pallas kernels: 28.6 us -> 27.2 us  [the longest x1 26.6 us: fused_device(): pl.pallas_call(functools.partial(fused_kernel, dp, mp), out_shape=tuple((...]
where the time goes in v5:
time: 28 us; the launch traced here: 27.9 us
  Pallas kernels  27.2 us (97%)
  between operations  0.64 us (2%)
    pallas_call x1, Pallas kernels, fused_device(): pl.pallas_call(functools.partial(fused_kernel, dp, mp), out_shape=tuple((...  26.6 us
    pallas_call x1, Pallas kernels, fused_device(): plain(*(pltpu.with_memory_space_constraint(held, pltpu.VMEM) for held in...  0.62 us

profile of v5, /device:TPU:0, one launch (start us, length us, event | category | flops | bytes accessed | tf_op | source)
XLA Modules:
  0.0 27.9 jit_solution(4775319730213351319)
XLA Ops:
  0.6 26.6 %shard_map.130 = (bf16[2,4608]{1,0:T(2,128)(2,1)S(1)}, bf16[1,2,8,128]{3,2,1,0:T(8,128)(2,1)S(1)}, bf16[1,2,8,128]{3,2,1,0:T(8,128)(2,1)S(1)}) custom-call(s32[2]{0:T(128)} %lengths_hbm.1, s32[1,2]{1,0:T(1,128)} %windowed_hbm.1, bf16[2,4608]{1,0:T(2,128)(2,1)} %hidden_hbm.1, f32[1,4608]{1,0:T(1,128)} %in_gain_hbm.1, f32[1,4608]{1,0:T(1,128)} %post_gain_hbm.1, ...), custom_call_target="tpu_custom_call" | custom-call | tf_op jit(solution)/shard_map/pallas_call | solution.py:548
  27.2 0.6 %shard_map.131 = (bf16[2,4608]{1,0:T(2,128)(2,1)}, bf16[1,2,8,128]{3,2,1,0:T(8,128)(2,1)}, bf16[1,2,8,128]{3,2,1,0:T(8,128)(2,1)}) custom-call(bf16[2,4608]{1,0:T(2,128)(2,1)S(1)} %get-tuple-element.6.a_ref, bf16[1,2,8,128]{3,2,1,0:T(8,128)(2,1)S(1)} %get-tuple-element.7.b_ref, bf16[1,2,8,128]{3,2,1,0:T(8,128)(2,1)S(1)} %get-tuple-element.8.c_ref), custom_call_target="tpu_custom_call" | custom-call | tf_op jit(solution)/shard_map/pallas_call | solution.py:598

commit v6 on v5

--- a/solution.py
+++ b/solution.py
@@ -443,12 +443,6 @@
     exchange(token_recv, 5, along_mp, lambda a, b: token_send, my_mp)
     token_recv[my_mp] = token_send[...]
 
-    gather = one_hot(
-        query_heads * total_rows,
-        query_heads * total_rows,
-        lambda row, column: column
-        == low(row, total_rows) * query_heads + high(row, total_rows),
-    )
     for load in loads[9:]:
         load.wait()
     finish(mix_recv, devices - 1, recv_sem.at[3])
@@ -460,11 +454,10 @@
     at_row = lax.broadcasted_iota(jnp.int32, mixed.shape, 1)
     at_lane = lax.broadcasted_iota(jnp.int32, mixed.shape, 2)
     sums = jnp.sum(jnp.where(at_row == at_lane, sums, 0.0), axis=-1, keepdims=True)
-    attended = (mixed / sums).reshape(dp * block, HEAD_DIM).astype(jnp.bfloat16)
-    heads = pick(gather, attended).astype(jnp.bfloat16)
+    attended = (mixed / sums).reshape(total_rows, query_heads, HEAD_DIM)
     heads = jnp.concatenate(
-        [heads[b * total_rows : (b + 1) * total_rows] for b in range(query_heads)], axis=1
-    )
+        [attended[:, b, :] for b in range(query_heads)], axis=1
+    ).astype(jnp.bfloat16)
     partial_cols = lax.dot_general(
         heads, out_w[...], over_last, preferred_element_type=jnp.float32
     )

time: 28 us -> 27.9 us (level)
  no operation moved by 1% of the time
where the time goes in v6:
time: 27.9 us; the launch traced here: 27.7 us
  Pallas kernels  27.1 us (97%)
  between operations  0.64 us (2%)
    pallas_call x1, Pallas kernels, fused_device(): pl.pallas_call(functools.partial(fused_kernel, dp, mp), out_shape=tuple((...  26.5 us
    pallas_call x1, Pallas kernels, fused_device(): plain(*(pltpu.with_memory_space_constraint(held, pltpu.VMEM) for held in...  0.62 us

profile of v6, /device:TPU:0, one launch (start us, length us, event | category | flops | bytes accessed | tf_op | source)
XLA Modules:
  0.0 27.7 jit_solution(17576990475130446125)
XLA Ops:
  0.6 26.5 %shard_map.130 = (bf16[2,4608]{1,0:T(2,128)(2,1)S(1)}, bf16[1,2,8,128]{3,2,1,0:T(8,128)(2,1)S(1)}, bf16[1,2,8,128]{3,2,1,0:T(8,128)(2,1)S(1)}) custom-call(s32[2]{0:T(128)} %lengths_hbm.1, s32[1,2]{1,0:T(1,128)} %windowed_hbm.1, bf16[2,4608]{1,0:T(2,128)(2,1)} %hidden_hbm.1, f32[1,4608]{1,0:T(1,128)} %in_gain_hbm.1, f32[1,4608]{1,0:T(1,128)} %post_gain_hbm.1, ...), custom_call_target="tpu_custom_call" | custom-call | tf_op jit(solution)/shard_map/pallas_call | solution.py:541
  27.1 0.6 %shard_map.131 = (bf16[2,4608]{1,0:T(2,128)(2,1)}, bf16[1,2,8,128]{3,2,1,0:T(8,128)(2,1)}, bf16[1,2,8,128]{3,2,1,0:T(8,128)(2,1)}) custom-call(bf16[2,4608]{1,0:T(2,128)(2,1)S(1)} %get-tuple-element.6.a_ref, bf16[1,2,8,128]{3,2,1,0:T(8,128)(2,1)S(1)} %get-tuple-element.7.b_ref, bf16[1,2,8,128]{3,2,1,0:T(8,128)(2,1)S(1)} %get-tuple-element.8.c_ref), custom_call_target="tpu_custom_call" | custom-call | tf_op jit(solution)/shard_map/pallas_call | solution.py:591
